TPU v7x, 512 devices: a whole 4x4x16 slice. The times are simulated.
512 devices in a mesh: rows: 64 (over x, y, z_hi, core), cols: 8 (over z_lo).
Axes of the slice: x: 4, y: 4, z: 16 (z_hi: 2, z_lo: 8; z = z_hi * 8 + z_lo), core: 2. Of those that a mesh axis runs over, the one named last changes fastest.
Arguments:
- homolog_embedding: bfloat16 [512, 1024, 256], P('rows', 'cols'), may hold values from -120 to 120
- couple_embedding: bfloat16 [1024, 1024, 128], P('rows', 'cols'), may hold values from -6 to 6
- homolog_standardize_factor: float32 [256], replicated, may hold values from 0.25 to 1.75
- first_factor_mapping: bfloat16 [256, 32], replicated, may hold values from -0.375 to 0.375
- second_factor_mapping: bfloat16 [256, 32], replicated, may hold values from -0.375 to 0.375
- contraction_to_couple_mapping: bfloat16 [1024, 128], replicated, may hold values from -4 to 4
- couple_standardize_factor: float32 [128], replicated, may hold values from 0.25 to 1.75
- widening_matrix: bfloat16 [128, 512], replicated, may hold values from -0.5 to 0.5
- narrowing_matrix: bfloat16 [512, 128], replicated, may hold values from -0.25 to 0.25
Outputs:
- pair_out: bfloat16 [1024, 1024, 128], P('rows', 'cols')
All inputs are finite; a program needn't handle non-finite values.
Results may differ from a plain program's by a relative error of at most 0.0064.
Values may be sent and summed in bfloat16 or wider, within the bound.
A program may use at most 64 MiB of HBM per device.

v0:
```python
import math

import jax
import jax.numpy as jnp
from jax import lax
from jax.sharding import PartitionSpec as P


def standardize_features(sampled_entries, gain_vector):
    floats = sampled_entries.astype(jnp.float32)
    average = jnp.mean(floats, axis=-1, keepdims=True)
    centred = floats - average
    variance = jnp.mean(centred * centred, axis=-1, keepdims=True)
    return centred * lax.rsqrt(variance + 1e-05) * gain_vector


def project_rows(sampled_entries, weights):
    unrolled_tensor = sampled_entries.reshape(-1, sampled_entries.shape[2])
    product = jnp.dot(unrolled_tensor, weights, preferred_element_type=jnp.float32).astype(
        jnp.bfloat16
    )
    return product.reshape(sampled_entries.shape[0], sampled_entries.shape[1], weights.shape[1])


def on_device(
    homolog_embedding,
    couple_embedding,
    homolog_standardize_factor,
    first_factor_mapping,
    second_factor_mapping,
    contraction_to_couple_mapping,
    couple_standardize_factor,
    widening_matrix,
    narrowing_matrix,
):
    standardized_tensor = standardize_features(
        homolog_embedding, homolog_standardize_factor
    ).astype(jnp.bfloat16)
    res_local = standardized_tensor.shape[1]
    width_outer = first_factor_mapping.shape[1]
    right_local = project_rows(standardized_tensor, second_factor_mapping)
    left_local = project_rows(standardized_tensor, first_factor_mapping)
    copies = jnp.tile(left_local, (1, lax.axis_size("cols"), 1))
    left_tile = lax.all_to_all(
        lax.all_to_all(copies, "cols", split_axis=1, concat_axis=1, tiled=True),
        "rows",
        split_axis=1,
        concat_axis=0,
        tiled=True,
    )
    right_panel = lax.all_gather(right_local, "rows", axis=0, tiled=True)
    sequences = left_tile.shape[0]
    tile_height = left_tile.shape[1]
    block = math.gcd(tile_height, 4)
    block_count = tile_height // block
    left_blocks = left_tile.reshape(sequences, block_count, block * width_outer).transpose(1, 0, 2)
    right_matrix = right_panel.reshape(sequences, res_local * width_outer)

    def project_block(left_block):
        outer_product = (
            lax.dot_general(
                left_block,
                right_matrix,
                (((0,), (0,)), ((), ())),
                preferred_element_type=jnp.float32,
            )
            / sequences
        )
        outer_product = outer_product.astype(jnp.bfloat16).reshape(
            block, width_outer, res_local, width_outer
        )
        outer_product = outer_product.transpose(0, 2, 1, 3).reshape(
            block * res_local, width_outer * width_outer
        )
        return jnp.dot(
            outer_product, contraction_to_couple_mapping, preferred_element_type=jnp.float32
        )

    update = lax.map(project_block, left_blocks).reshape(
        tile_height, res_local, contraction_to_couple_mapping.shape[1]
    )
    pair_mid = couple_embedding.astype(jnp.float32) + update
    pair_normed = (
        standardize_features(pair_mid, couple_standardize_factor)
        .astype(jnp.bfloat16)
        .reshape(-1, couple_embedding.shape[2])
    )
    hidden = jnp.maximum(
        jnp.dot(pair_normed, widening_matrix, preferred_element_type=jnp.float32), 0.0
    ).astype(jnp.bfloat16)
    result = pair_mid + jnp.dot(
        hidden, narrowing_matrix, preferred_element_type=jnp.float32
    ).reshape(couple_embedding.shape)
    return result.astype(jnp.bfloat16)


def solution(mesh):
    return jax.shard_map(
        on_device,
        mesh=mesh,
        in_specs=(
            P("rows", "cols", None),
            P("rows", "cols", None),
            P(),
            P(),
            P(),
            P(),
            P(),
            P(),
            P(),
        ),
        out_specs=P("rows", "cols", None),
        check_vma=False,
    )
```

profile of v0, /device:TPU:1, one launch (start us, length us, event | category | flops | bytes accessed | tf_op | source)
XLA Modules:
  0.0 234.6 jit_solution(8320753588659107767)
XLA Ops:
  6.5 0.0 copy-start
  6.5 0.0 copy-start.2
  6.5 0.0 copy-start.3
  6.5 0.0 all-gather.2.cloned.1.call-start
  6.5 1.3 convert_reduce_fusion
  7.9 1.4 fusion.12
  9.3 1.4 fusion.14
  10.7 0.0 copy-done.2
  10.7 0.2 fusion.11
  10.9 0.7 copy.40
  11.6 0.0 all-gather.2.cloned.1.call-update
  11.6 0.0 copy-done.3
  11.6 0.2 fusion.10
  11.9 0.2 copy.24
  12.1 0.3 tile.11
  12.4 2.0 reshape.66
  14.4 39.6 %all_to_all.20 = bf16[8,2,16384]{2,1,0:T(2,128)(2,1)S(1)} all-to-all(bf16[8,2,16384]{2,1,0:T(2,128)(2,1)S(1)} %reshape.66), channel_id=1, replica_groups=mesh['rows'=64,'cols'=8] {'cols'}, dimensions={0} | all-to-all | bytes 1048576 | tf_op jit(solution)/shard_map/all_to_all | solution.py:45
  53.9 1.0 reshape.67
  55.0 1.5 bitcast_bitcast_fusion
  56.4 4.5 %reshape.68 = bf16[64,2,2048]{2,1,0:T(2,128)(2,1)} reshape(bf16[1024,8,32]{2,1,0:T(8,128)(2,1)} %bitcast_bitcast_fusion) | data formatting | bytes 1048576
  60.9 18.2 %all-to-all-start.1 = ((bf16[64,2,2048]{2,1,0:T(2,128)(2,1)}), bf16[64,2,2048]{2,1,0:T(2,128)(2,1)}, u32[]{:S(2)}, u32[]{:S(2)}) async-start(bf16[64,2,2048]{2,1,0:T(2,128)(2,1)} %reshape.68), calls=%async_computation.1 | async-start | bytes 1048576 | tf_op jit(solution)/shard_map/all_to_all | solution.py:44
  79.1 35.0 %all-to-all-done.1 = bf16[64,2,2048]{2,1,0:T(2,128)(2,1)} async-done(((bf16[64,2,2048]{2,1,0:T(2,128)(2,1)}), bf16[64,2,2048]{2,1,0:T(2,128)(2,1)}, u32[]{:S(2)}, u32[]{:S(2)}) %all-to-all-start.1) | async-done | bytes 524320 | tf_op jit(solution)/shard_map/all_to_all | solution.py:44
  114.1 3.0 %reshape.69 = bf16[1024,8,32]{2,1,0:T(8,128)(2,1)S(1)} reshape(bf16[64,2,2048]{2,1,0:T(2,128)(2,1)} %all-to-all-done.1) | data formatting | bytes 1048576
  117.2 1.9 copy.26
  119.1 3.1 %reshape.60 = bf16[512,4,128]{2,1,0:T(4,128)(2,1)S(1)} reshape(bf16[64,8,16,32]{3,2,1,0:T(8,128)(2,1)} %copy.26) | data formatting | bytes 1048576 | tf_op jit(solution)/shard_map/reshape | solution.py:56
  122.2 0.1 copy.29
  122.3 40.2 %all-gather.2.cloned.1.call-done = bf16[512,128,32]{1,2,0:T(8,128)(2,1)} async-done(((bf16[8,128,32]{1,2,0:T(8,128)(2,1)}), bf16[512,128,32]{1,2,0:T(8,128)(2,1)}) %all-gather.2.cloned.1.call-update) | async-done | bytes 4194320 | tf_op jit(solution)/shard_map/all_gather | solution.py:51
  162.5 8.6 %copy.28 = bf16[512,128,32]{0,2,1:T(8,128)(2,1)} copy(bf16[512,128,32]{1,2,0:T(8,128)(2,1)} %all-gather.2.cloned.1.call-done) | data formatting | bytes 8388608 | tf_op jit(solution)/shard_map/all_gather | solution.py:51
  171.1 0.0 copy-start.5
  171.1 6.4 %copy.30 = bf16[512,4096]{1,0:T(8,128)(2,1)} copy(bf16[512,4096]{0,1:T(8,128)(2,1)} %bitcast.72) | data formatting | bytes 8388608 | tf_op jit(solution)/shard_map/while | solution.py:79
  177.5 0.0 copy-done.5
  177.5 0.0 copy-start.1
  177.5 46.2 %while.10 = (s32[]{:T(128)}, f32[4,512,128]{2,1,0:T(8,128)S(1)}, bf16[4,512,128]{2,1,0:T(8,128)(2,1)S(1)}, bf16[512,4096]{1,0:T(8,128)(2,1)}, bf16[1024,128]{1,0:T(8,128)(2,1)S(1)}, /*index=5*/s32[]{:T(128)}) while((s32[]{:T(128)}, f32[4,512,128]{2,1,0:T(8,128)S(1)}, bf16[4,512,128]{2,1,0:T(8,128)(2,1)S(1)}, bf16[512,4096]{1,0:T(8,128)(2,1)}, ...), condition=%wide.region_3.4_spmd, body=%wide.region_2.3_spmd.sunk | while | flops 672137216 | bytes 11141197 | solution.py:79
  177.5 3.0 %fusion.36 = bf16[128,4096]{1,0:T(8,128)(2,1)S(1)} fusion(bf16[512,4096]{1,0:T(8,128)(2,1)} %get-tuple-element.104, bf16[4,512,128]{2,1,0:T(8,128)(2,1)S(1)} %get-tuple-element.103, s32[]{:T(128)} %get-tuple-element.95), kind=kOutput, calls=%fused_computation.1.clone.1 | convolution fusion | flops 537919488 | bytes 5373956 | tf_op jit(solution)/shard_map/while/body/eval_jaxpr/dot_general | solution.py:61
  180.5 4.4 %reshape.71 = bf16[4,32,128,32]{3,2,1,0:T(8,128)(2,1)} reshape(bf16[128,4096]{1,0:T(8,128)(2,1)S(1)} %fusion.36) | data formatting | bytes 2097152 | tf_op jit(solution)/shard_map/while/body/eval_jaxpr/reshape | solution.py:69
  184.9 3.7 %copy.44 = bf16[4,128,32,32]{1,0,3,2:T(4,128)(2,1)S(1)} copy(bf16[4,128,32,32]{3,1,2,0:T(8,128)(2,1)} %bitcast.66) | data formatting | bytes 2097152 | tf_op jit(solution)/shard_map/while/body/eval_jaxpr/transpose | solution.py:72
  188.6 0.5 fusion.37
  189.1 2.9 %fusion.36 = bf16[128,4096]{1,0:T(8,128)(2,1)S(1)} fusion(bf16[512,4096]{1,0:T(8,128)(2,1)} %get-tuple-element.104, bf16[4,512,128]{2,1,0:T(8,128)(2,1)S(1)} %get-tuple-element.103, s32[]{:T(128)} %get-tuple-element.95), kind=kOutput, calls=%fused_computation.1.clone.1 | convolution fusion | flops 537919488 | bytes 5373956 | tf_op jit(solution)/shard_map/while/body/eval_jaxpr/dot_general | solution.py:61
  192.1 4.4 %reshape.71 = bf16[4,32,128,32]{3,2,1,0:T(8,128)(2,1)} reshape(bf16[128,4096]{1,0:T(8,128)(2,1)S(1)} %fusion.36) | data formatting | bytes 2097152 | tf_op jit(solution)/shard_map/while/body/eval_jaxpr/reshape | solution.py:69
  196.5 3.7 %copy.44 = bf16[4,128,32,32]{1,0,3,2:T(4,128)(2,1)S(1)} copy(bf16[4,128,32,32]{3,1,2,0:T(8,128)(2,1)} %bitcast.66) | data formatting | bytes 2097152 | tf_op jit(solution)/shard_map/while/body/eval_jaxpr/transpose | solution.py:72
  200.1 0.5 fusion.37
  200.7 2.9 %fusion.36 = bf16[128,4096]{1,0:T(8,128)(2,1)S(1)} fusion(bf16[512,4096]{1,0:T(8,128)(2,1)} %get-tuple-element.104, bf16[4,512,128]{2,1,0:T(8,128)(2,1)S(1)} %get-tuple-element.103, s32[]{:T(128)} %get-tuple-element.95), kind=kOutput, calls=%fused_computation.1.clone.1 | convolution fusion | flops 537919488 | bytes 5373956 | tf_op jit(solution)/shard_map/while/body/eval_jaxpr/dot_general | solution.py:61
  203.6 4.4 %reshape.71 = bf16[4,32,128,32]{3,2,1,0:T(8,128)(2,1)} reshape(bf16[128,4096]{1,0:T(8,128)(2,1)S(1)} %fusion.36) | data formatting | bytes 2097152 | tf_op jit(solution)/shard_map/while/body/eval_jaxpr/reshape | solution.py:69
  208.0 3.7 %copy.44 = bf16[4,128,32,32]{1,0,3,2:T(4,128)(2,1)S(1)} copy(bf16[4,128,32,32]{3,1,2,0:T(8,128)(2,1)} %bitcast.66) | data formatting | bytes 2097152 | tf_op jit(solution)/shard_map/while/body/eval_jaxpr/transpose | solution.py:72
  211.7 0.5 fusion.37
  212.2 2.9 %fusion.36 = bf16[128,4096]{1,0:T(8,128)(2,1)S(1)} fusion(bf16[512,4096]{1,0:T(8,128)(2,1)} %get-tuple-element.104, bf16[4,512,128]{2,1,0:T(8,128)(2,1)S(1)} %get-tuple-element.103, s32[]{:T(128)} %get-tuple-element.95), kind=kOutput, calls=%fused_computation.1.clone.1 | convolution fusion | flops 537919488 | bytes 5373956 | tf_op jit(solution)/shard_map/while/body/eval_jaxpr/dot_general | solution.py:61
  215.1 4.4 %reshape.71 = bf16[4,32,128,32]{3,2,1,0:T(8,128)(2,1)} reshape(bf16[128,4096]{1,0:T(8,128)(2,1)S(1)} %fusion.36) | data formatting | bytes 2097152 | tf_op jit(solution)/shard_map/while/body/eval_jaxpr/reshape | solution.py:69
  219.6 3.7 %copy.44 = bf16[4,128,32,32]{1,0,3,2:T(4,128)(2,1)S(1)} copy(bf16[4,128,32,32]{3,1,2,0:T(8,128)(2,1)} %bitcast.66) | data formatting | bytes 2097152 | tf_op jit(solution)/shard_map/while/body/eval_jaxpr/transpose | solution.py:72
  223.2 0.5 fusion.37
  223.7 0.0 copy-start.4
  223.8 0.0 copy-done.1
  223.8 0.3 fusion.15
  224.1 0.0 copy-start.6
  224.1 0.7 multiply_reduce_fusion
  224.8 0.0 copy-done.4
  224.8 0.7 multiply_convert_fusion
  225.6 0.0 copy-done
  225.6 0.0 copy-done.6
  225.6 1.2 fusion.7
  226.8 1.0 add_convert_fusion
  (6 shorter events, 0.1 us)
Async XLA Ops:
  6.5 219.0 %copy-start = (bf16[512,128]{1,0:T(8,128)(2,1)S(1)}, bf16[512,128]{1,0:T(8,128)(2,1)}, u32[]{:S(2)}) copy-start(bf16[512,128]{1,0:T(8,128)(2,1)} %param.19) | copy-start | bytes 393220
  6.5 4.1 %copy-start.2 = (bf16[256,32]{0,1:T(8,128)(2,1)S(1)}, bf16[256,32]{0,1:T(8,128)(2,1)}, u32[]{:S(2)}) copy-start(bf16[256,32]{0,1:T(8,128)(2,1)} %param.15) | copy-start | bytes 49156
  6.5 5.1 %copy-start.3 = (bf16[256,32]{0,1:T(8,128)(2,1)S(1)}, bf16[256,32]{0,1:T(8,128)(2,1)}, u32[]{:S(2)}) copy-start(bf16[256,32]{0,1:T(8,128)(2,1)} %param.14) | copy-start | bytes 49156
  6.5 155.9 %all-gather.2.cloned.1.call-start = ((), (), s32[]{:S(2)}) async-start(), calls=%async_computation.2 | async-start | bytes 4259840 | tf_op jit(solution)/shard_map/all_gather | solution.py:51
  60.9 53.3 %all-to-all-start.1 = ((bf16[64,2,2048]{2,1,0:T(2,128)(2,1)}), bf16[64,2,2048]{2,1,0:T(2,128)(2,1)}, u32[]{:S(2)}, u32[]{:S(2)}) async-start(bf16[64,2,2048]{2,1,0:T(2,128)(2,1)} %reshape.68), calls=%async_computation.1 | async-start | bytes 1048576 | tf_op jit(solution)/shard_map/all_to_all | solution.py:44
  171.1 6.4 %copy-start.5 = (bf16[1024,128]{1,0:T(8,128)(2,1)S(1)}, bf16[1024,128]{1,0:T(8,128)(2,1)}, u32[]{:S(2)}) copy-start(bf16[1024,128]{1,0:T(8,128)(2,1)} %param.16) | copy-start | bytes 786436
  177.5 46.2 %copy-start.1 = (bf16[16,128,128]{2,1,0:T(8,128)(2,1)S(1)}, bf16[16,128,128]{2,1,0:T(8,128)(2,1)}, u32[]{:S(2)}) copy-start(bf16[16,128,128]{2,1,0:T(8,128)(2,1)} %param.12) | copy-start | bytes 1572868
  223.7 1.1 copy-start.4
  224.1 1.4 copy-start.6
Sparse Core Ops, SparseCore 0:
  11.7 150.7 all-gather.1
where the time goes:
time: 236 us; the launch traced here: 235 us
  waiting for transfers between devices  75.2 us (32%)
  local copies, waits for them, and re-layouts  65.6 us (28%)
  blocking collectives  39.6 us (17%)
  starting transfers between devices  18.3 us (8%)
  matrix products  15.5 us (7%)
  between operations  13.6 us (6%)
  other arithmetic  6.79 us (3%)
    all_gather x1, waiting for transfers between devices, on_device(): right_panel = lax.all_gather(right_local, 'rows', axis=0, tiled=True)  40.2 us
    all_to_all x1, blocking collectives, on_device(): lax.all_to_all(copies, 'cols', split_axis=1, concat_axis=1, tiled=True)  39.6 us
    all_to_all x1, waiting for transfers between devices, on_device(): lax.all_to_all(lax.all_to_all(copies, 'cols', split_axis=1, concat_axis=1...  35 us
    all_to_all x1, starting transfers between devices, on_device(): lax.all_to_all(lax.all_to_all(copies, 'cols', split_axis=1, concat_axis=1...  18.2 us
    reshape x4, local copies, waits for them, and re-layouts, project_block(): outer_product.astype(jnp.bfloat16)  17.7 us
    transpose x4, local copies, waits for them, and re-layouts, project_block(): outer_product.transpose(0, 2, 1, 3)  14.6 us
    unnamed x20, local copies, waits for them, and re-layouts  12 us
    dot_general x4, matrix products, project_block(): lax.dot_general(left_block, right_matrix, (((0,), (0,)), ((), ())), prefe...  11.8 us
  transfers between devices with their start and end apart: 2, of which 2 were waited for; matrix products, arithmetic and copies ran while one was open for 8% of the time, Pallas kernels for 0%

commit v1 on v0

v1 whole, which is shorter than its diff:
```python
import jax
import jax.numpy as jnp
from jax import lax
from jax.experimental import pallas as pl
from jax.experimental.pallas import tpu as pltpu
from jax.sharding import PartitionSpec as P

MESH = pl.DeviceIdType.MESH
F32 = jnp.float32
BF16 = jnp.bfloat16
EPS = 1e-5


def kernel(
    x_ref,
    cpl_hbm,
    g1_ref,
    w1_ref,
    w2_ref,
    w3_hbm,
    g2_ref,
    wa_hbm,
    wb_hbm,
    out_ref,
    cpl_ref,
    w3_ref,
    wa_ref,
    wb_ref,
    w3f_ref,
    wt_ref,
    xn_ref,
    tf_ref,
    lx_ref,
    rx_ref,
    xl_ref,
    xr_ref,
    lloc_ref,
    lz_ref,
    lb_ref,
    lt_ref,
    rb_ref,
    oall_ref,
    in_sem,
    xsend,
    xrecv,
    rsend,
    rrecv,
    sibsend,
    sibrecv,
    zsend,
    zrecv,
    psend,
    precv,
):
    r = lax.axis_index("rows")
    zl = lax.axis_index("cols")
    core = r % 2
    zh = (r // 2) % 2
    y = (r // 4) % 4
    x = r // 16
    z = zh * 8 + zl

    def rows_of(xx, yy, hh, kk):
        return ((xx * 4 + yy) * 2 + hh) * 2 + kk

    sib = (rows_of(x, y, zh, 1 - core), zl)

    def plane(d):
        px = (x + d // 4) % 4
        py = (y + d % 4) % 4
        return px, py

    def zdev(dz):
        zz = (z + dz) % 16
        return (rows_of(x, y, zz // 8, core), zz % 8)

    barrier = pltpu.get_barrier_semaphore()
    pl.semaphore_signal(barrier, inc=1, device_id=sib, device_id_type=MESH)

    def greet_plane(d, _):
        px, py = plane(d)
        pl.semaphore_signal(
            barrier, inc=1, device_id=(rows_of(px, py, zh, core), zl), device_id_type=MESH
        )
        return 0

    lax.fori_loop(1, 16, greet_plane, 0)

    def greet_z(d, _):
        pl.semaphore_signal(barrier, inc=1, device_id=zdev(d), device_id_type=MESH)
        return 0

    lax.fori_loop(1, 16, greet_z, 0)

    loads = [
        pltpu.make_async_copy(src, dst, in_sem.at[n])
        for n, (src, dst) in enumerate(
            [(w3_hbm, w3_ref), (cpl_hbm, cpl_ref), (wa_hbm, wa_ref), (wb_hbm, wb_ref)]
        )
    ]
    for load in loads:
        load.start()

    gain = g1_ref[...]
    for s in range(8):
        xs = x_ref[s].astype(F32)
        mean = jnp.mean(xs, axis=-1, keepdims=True)
        cen = xs - mean
        var = jnp.mean(cen * cen, axis=-1, keepdims=True)
        xn_ref[s * 128 : (s + 1) * 128, :] = (cen * lax.rsqrt(var + EPS) * gain).astype(BF16)
    w1 = w1_ref[...]
    w2 = w2_ref[...]
    wcat = jnp.concatenate([w1] * 4 + [w2] * 4, axis=1)
    for s in range(8):
        both = jnp.dot(xn_ref[s * 128 : (s + 1) * 128, :], wcat, preferred_element_type=F32)
        tf_ref[pl.ds(s, 128, stride=8), :] = both[:, :128]
        right = both[:, 128:].T
        rx_ref[pl.ds(s, 32, stride=8), :] = right[:32]
    lane = lax.broadcasted_iota(jnp.int32, (8, 128), 1) // 32
    for kk in range(2):
        for hh in range(2):
            for yy in range(2):
                gg = yy * 4 + hh * 2 + kk
                for g in range(4):
                    base = (gg * 16 + g * 4) * 8
                    tile = tf_ref[base : base + 8, :]
                    for e in range(1, 4):
                        other = tf_ref[base + e * 8 : base + e * 8 + 8, :]
                        tile = jnp.where(lane == e, other, tile)
                    lx_ref[kk, hh * 2 + yy, :, g * 128 : (g + 1) * 128] = tile

    pl.semaphore_wait(barrier, 31)

    def swap(n):
        if n == 0:
            src, dst = rx_ref.at[pl.ds(pl.multiple_of((1 - core) * 128, 128), 128)], xr_ref.at[core]
        else:
            src, dst = lx_ref.at[1 - core], xl_ref.at[core]
        return pltpu.make_async_remote_copy(
            src_ref=src,
            dst_ref=dst,
            send_sem=xsend.at[n],
            recv_sem=xrecv.at[n],
            device_id=sib,
            device_id_type=MESH,
        )

    def swap_in(n):
        dst = xr_ref.at[1 - core] if n == 0 else xl_ref.at[1 - core]
        return pltpu.make_async_remote_copy(
            src_ref=dst,
            dst_ref=dst,
            send_sem=xsend.at[n],
            recv_sem=xrecv.at[n],
            device_id=sib,
            device_id_type=MESH,
        )

    swap(0).start()
    swap(1).start()
    xr_ref[core] = rx_ref[pl.ds(pl.multiple_of(core * 128, 128), 128), :]
    xl_ref[core] = lx_ref[core]
    mine = zh * 16 + x * 4 + y
    swap_in(0).wait_recv()
    for q in range(16):
        rb_ref[core, mine, :, q * 128 : (q + 1) * 128] = jnp.concatenate(
            [xr_ref[0, q * 8 : (q + 1) * 8, :], xr_ref[1, q * 8 : (q + 1) * 8, :]], axis=0
        ).astype(BF16)

    def rcopy(slot, dev, sem):
        return pltpu.make_async_remote_copy(
            src_ref=rb_ref.at[core, slot],
            dst_ref=rb_ref.at[core, slot],
            send_sem=rsend.at[sem],
            recv_sem=rrecv.at[slot],
            device_id=dev,
            device_id_type=MESH,
        )

    def scopy(slot, half):
        return pltpu.make_async_remote_copy(
            src_ref=rb_ref.at[half, slot],
            dst_ref=rb_ref.at[half, slot],
            send_sem=sibsend.at[slot],
            recv_sem=sibrecv.at[slot],
            device_id=sib,
            device_id_type=MESH,
        )

    partner = (1 - zh) * 16 + x * 4 + y
    zpart = (rows_of(x, y, 1 - zh, core), zl)

    def adev(e):
        return (rows_of((x + e * (1 - core)) % 4, (y + e * core) % 4, zh, core), zl)

    def bdev(e):
        return (rows_of((x + e * core) % 4, (y + e * (1 - core)) % 4, zh, core), zl)

    def aslot(e, hh):
        return hh * 16 + ((x + (4 - e) * (1 - core)) % 4) * 4 + (y + (4 - e) * core) % 4

    def send_a(hh, base):
        def body(e, _):
            rcopy(aslot(0, hh), adev(e), base + e - 1).start()
            return 0

        lax.fori_loop(1, 4, body, 0)

    def send_b(hh, base, a):
        def body(e, _):
            rcopy(aslot(a, hh), bdev(e), base + a * 3 + e - 1).start()
            return 0

        lax.fori_loop(1, 4, body, 0)

    rcopy(mine, zpart, 0).start()
    send_a(zh, 1)
    send_b(zh, 7, 0)

    swap_in(1).wait_recv()
    for hy in range(4):
        for g in range(4):
            cols = slice(g * 128, (g + 1) * 128)
            lloc_ref[hy // 2, hy % 2, :, cols] = jnp.concatenate(
                [xl_ref[0, hy, :, cols], xl_ref[1, hy, :, cols]], axis=0
            ).astype(BF16)

    def zcopy(dz):
        zz = (z + dz) % 16
        return pltpu.make_async_remote_copy(
            src_ref=lloc_ref.at[zz // 8],
            dst_ref=lz_ref.at[z],
            send_sem=zsend.at[dz],
            recv_sem=zrecv.at[z],
            device_id=zdev(dz),
            device_id_type=MESH,
        )

    def zcopy_in(zz):
        return pltpu.make_async_remote_copy(
            src_ref=lz_ref.at[zz],
            dst_ref=lz_ref.at[zz],
            send_sem=zsend.at[0],
            recv_sem=zrecv.at[zz],
            device_id=zdev(1),
            device_id_type=MESH,
        )

    def zstart(n, _):
        dz = (8 + ((n + 1) // 2) * (1 - 2 * (n % 2)) + 16) % 16
        zcopy(dz).start()
        return 0

    lax.fori_loop(0, 15, zstart, 0)
    lz_ref[z] = lloc_ref[zh]
    scopy(mine, core).start()

    def fwd_a(hh, base):
        def body(e, _):
            slot = aslot(e, hh)
            rcopy(slot, adev(1), 0).wait_recv()
            send_b(hh, base, e)
            scopy(slot, core).start()
            return 0

        lax.fori_loop(1, 4, body, 0)

    fwd_a(zh, 7)

    loads[0].wait()
    for p in range(32):
        w3f_ref[pl.ds(p, 32, stride=32), :] = w3_ref[p * 32 : (p + 1) * 32, :].astype(F32)
    for n in range(8):
        wt_ref[:, n * 128 : (n + 1) * 128] = w3f_ref[n * 128 : (n + 1) * 128, :].T.astype(BF16)

    rcopy(partner, zpart, 0).wait_recv()
    send_a(1 - zh, 4)
    send_b(1 - zh, 19, 0)
    scopy(partner, core).start()
    fwd_a(1 - zh, 19)

    def pcopy(d, hh):
        px, py = plane(d)
        return pltpu.make_async_remote_copy(
            src_ref=lz_ref.at[hh * 8 + px * 2 + py // 2, py % 2],
            dst_ref=lb_ref.at[hh * 16 + x * 4 + y],
            send_sem=psend.at[d * 2 + hh],
            recv_sem=precv.at[hh * 16 + x * 4 + y],
            device_id=(rows_of(px, py, zh, core), zl),
            device_id_type=MESH,
        )

    def pcopy_in(slot):
        return pltpu.make_async_remote_copy(
            src_ref=lb_ref.at[slot],
            dst_ref=lb_ref.at[slot],
            send_sem=psend.at[0],
            recv_sem=precv.at[slot],
            device_id=sib,
            device_id_type=MESH,
        )

    def zwait(dz, _):
        zcopy_in((z + dz) % 16).wait_recv()
        return 0

    lax.fori_loop(1, 16, zwait, 0)

    def pstart(d, _):
        for hh in range(2):
            pcopy(d, hh).start()
        return 0

    lax.fori_loop(1, 16, pstart, 0)
    for hh in range(2):
        lb_ref[hh * 16 + x * 4 + y] = lz_ref[hh * 8 + x * 2 + y // 2, y % 2]

    def bslot(n, hh):
        e = n // 4 + 1
        a = n % 4
        return (
            hh * 16
            + ((x + (4 - a) * (1 - core) + (4 - e) * core) % 4) * 4
            + (y + (4 - a) * core + (4 - e) * (1 - core)) % 4
        )

    def fwd_sib(hh):
        def body(n, _):
            slot = bslot(n, hh)
            rcopy(slot, adev(1), 0).wait_recv()
            scopy(slot, core).start()
            return 0

        lax.fori_loop(0, 12, body, 0)

    fwd_sib(zh)
    fwd_sib(1 - zh)

    def pwait(d, _):
        px, py = plane(d)
        for hh in range(2):
            pcopy_in(hh * 16 + px * 4 + py).wait_recv()
        return 0

    lax.fori_loop(1, 16, pwait, 0)
    for n in range(4):
        for m in range(4):
            lt_ref[m * 128 : (m + 1) * 128, n * 128 : (n + 1) * 128] = (
                lb_ref[n * 8 : (n + 1) * 8, :, m * 128 : (m + 1) * 128].reshape(128, 128).T
            )

    def sibwait(slot, _):
        scopy(slot, 1 - core).wait_recv()
        return 0

    lax.fori_loop(0, 32, sibwait, 0)

    for h in range(2):

        def outer(qb, _, h=h):
            off = pl.multiple_of(qb * 256, 256)
            right = rb_ref[h, :, :, pl.ds(off, 256)].reshape(512, 256)
            prod = jnp.dot(lt_ref[...], right, preferred_element_type=F32).astype(BF16)
            row = pl.multiple_of((h * 16 + qb * 2) * 32, 64)
            for i in range(16):
                for q in range(2):
                    oall_ref[
                        i // 2, pl.ds(row + q * 32, 32), (i % 2) * 128 : (i % 2 + 1) * 128
                    ] = prod[i * 32 : (i + 1) * 32, q * 128 : (q + 1) * 128]
            return 0

        lax.fori_loop(0, 8, outer, 0)

    for load in loads[1:]:
        load.wait()
    gain2 = g2_ref[...]

    def finish(n, _):
        for m in range(2):
            up = jnp.dot(wt_ref[...], oall_ref[n * 2 + m], preferred_element_type=F32)
            mids = []
            for k in range(2):
                i = n * 4 + m * 2 + k
                mids.append(
                    cpl_ref[i].astype(F32) + up[:, k * 128 : (k + 1) * 128].T * (1.0 / 512.0)
                )
            mid = jnp.concatenate(mids, axis=0)
            mean = jnp.mean(mid, axis=-1, keepdims=True)
            cen = mid - mean
            var = jnp.mean(cen * cen, axis=-1, keepdims=True)
            normed = (cen * lax.rsqrt(var + EPS) * gain2).astype(BF16)
            hidden = jnp.maximum(
                jnp.dot(normed, wa_ref[...], preferred_element_type=F32), 0.0
            ).astype(BF16)
            res = mid + jnp.dot(hidden, wb_ref[...], preferred_element_type=F32)
            out_ref[pl.ds(n * 4 + m * 2, 2)] = res.astype(BF16).reshape(2, 128, 128)
        return 0

    lax.fori_loop(0, 4, finish, 0)

    swap(0).wait_send()
    swap(1).wait_send()

    def rsent(n, _):
        rcopy(mine, zpart, n).wait_send()
        return 0

    lax.fori_loop(0, 31, rsent, 0)

    def sibsent(n, _):
        scopy(n, core).wait_send()
        return 0

    lax.fori_loop(0, 32, sibsent, 0)

    def zsent(n, _):
        zcopy(n).wait_send()
        return 0

    lax.fori_loop(1, 16, zsent, 0)

    def psent(n, _):
        for hh in range(2):
            pcopy(n, hh).wait_send()
        return 0

    lax.fori_loop(1, 16, psent, 0)


def on_device(x, cpl, g1, w1, w2, w3, g2, wa, wb):
    vmem = pl.BlockSpec(memory_space=pltpu.VMEM)
    hbm = pl.BlockSpec(memory_space=pl.ANY)
    dma = pltpu.SemaphoreType.DMA
    return pl.pallas_call(
        kernel,
        out_shape=jax.ShapeDtypeStruct(cpl.shape, BF16),
        in_specs=[vmem, hbm, vmem, vmem, vmem, hbm, vmem, hbm, hbm],
        out_specs=vmem,
        scratch_shapes=[
            pltpu.VMEM((16, 128, 128), BF16),
            pltpu.VMEM((1024, 128), BF16),
            pltpu.VMEM((128, 512), BF16),
            pltpu.VMEM((512, 128), BF16),
            pltpu.VMEM((1024, 128), F32),
            pltpu.VMEM((128, 1024), BF16),
            pltpu.VMEM((1024, 256), BF16),
            pltpu.VMEM((1024, 128), F32),
            pltpu.VMEM((2, 4, 8, 512), F32),
            pltpu.VMEM((256, 128), F32),
            pltpu.VMEM((2, 4, 8, 512), F32),
            pltpu.VMEM((2, 128, 128), F32),
            pltpu.VMEM((2, 2, 16, 512), BF16),
            pltpu.VMEM((16, 2, 16, 512), BF16),
            pltpu.VMEM((32, 16, 512), BF16),
            pltpu.VMEM((512, 512), BF16),
            pltpu.VMEM((2, 32, 16, 2048), BF16),
            pltpu.VMEM((8, 1024, 256), BF16),
            dma((4,)),
            dma((2,)),
            dma((2,)),
            dma((31,)),
            dma((32,)),
            dma((32,)),
            dma((32,)),
            dma((16,)),
            dma((16,)),
            dma((32,)),
            dma((32,)),
        ],
        compiler_params=pltpu.CompilerParams(
            collective_id=0, has_side_effects=True, vmem_limit_bytes=48 * 1024 * 1024
        ),
    )(x, cpl, g1.reshape(1, 256), w1, w2, w3, g2.reshape(1, 128), wa, wb)


def solution(mesh):
    return jax.shard_map(
        on_device,
        mesh=mesh,
        in_specs=(
            P("rows", "cols", None),
            P("rows", "cols", None),
            P(),
            P(),
            P(),
            P(),
            P(),
            P(),
            P(),
        ),
        out_specs=P("rows", "cols", None),
        check_vma=False,
    )
```

time: 236 us -> 80.7 us (0.34)
  waiting for transfers between devices: 75.2 us -> 0 us
  Pallas kernels: 0 us -> 73.9 us
  local copies, waits for them, and re-layouts: 65.6 us -> 6.46 us
  blocking collectives: 39.6 us -> 0 us
  starting transfers between devices: 18.3 us -> 0 us
  matrix products: 15.5 us -> 0 us
  between operations: 13.6 us -> 0.06 us
  other arithmetic: 6.79 us -> 0 us
    pallas_call x0 -> x1, Pallas kernels: none -> 73.9 us  [on_device(): pl.pallas_call(kernel, out_shape=jax.ShapeDtypeStruct(cpl.shape, BF16), i...]
    all_gather x1 -> x0, waiting for transfers between devices: 40.2 us -> none  [on_device(): right_panel = lax.all_gather(right_local, 'rows', axis=0, tiled=True)]
    all_to_all x1 -> x0, blocking collectives: 39.6 us -> none  [on_device(): lax.all_to_all(copies, 'cols', split_axis=1, concat_axis=1, tiled=True)]
    all_to_all x1 -> x0, waiting for transfers between devices: 35 us -> none  [on_device(): lax.all_to_all(lax.all_to_all(copies, 'cols', split_axis=1, concat_axis=1...]
    reshape x6 -> x0, local copies, waits for them, and re-layouts: 21.5 us -> none  [the longest x4 17.7 us: project_block(): outer_product.astype(jnp.bfloat16)]
    all_to_all x1 -> x0, starting transfers between devices: 18.2 us -> none  [on_device(): lax.all_to_all(lax.all_to_all(copies, 'cols', split_axis=1, concat_axis=1...]
    dot_general x11 -> x0, matrix products: 15.5 us -> none  [the longest x4 11.8 us: project_block(): lax.dot_general(left_block, right_matrix, (((0,), (0,)), ((), ())), prefe...]
    transpose x4 -> x0, local copies, waits for them, and re-layouts: 14.6 us -> none  [project_block(): outer_product.transpose(0, 2, 1, 3)]
  transfers between devices with their start and end apart: 2 -> 0, of which waited for: 2 -> 0; matrix products, arithmetic and copies ran while one was open for 8% -> 0% of each run, Pallas kernels for 0% -> 0%
where the time goes in v1:
time: 80.7 us; the launch traced here: 80.4 us
  Pallas kernels  73.9 us (92%)
  local copies, waits for them, and re-layouts  6.46 us (8%)
    pallas_call x1, Pallas kernels, on_device(): pl.pallas_call(kernel, out_shape=jax.ShapeDtypeStruct(cpl.shape, BF16), i...  73.9 us
    unnamed x17, local copies, waits for them, and re-layouts  6.46 us

profile of v1, /device:TPU:1, one launch (start us, length us, event | category | flops | bytes accessed | tf_op | source)
XLA Modules:
  0.0 80.4 jit_solution(3909165819301252659)
XLA Ops:
  0.0 0.0 copy-start.3
  0.0 0.9 %copy.10.w1_ref = bf16[256,32]{1,0:T(8,128)(2,1)S(1)} copy(bf16[256,32]{0,1:T(8,128)(2,1)} %param.12) | data formatting | bytes 32768 | tf_op args[3]
  0.9 0.0 copy-start.5
  0.9 0.0 copy-start.6
  0.9 0.8 %copy.11.w2_ref = bf16[256,32]{1,0:T(8,128)(2,1)S(1)} copy(bf16[256,32]{0,1:T(8,128)(2,1)} %param.13) | data formatting | bytes 32768 | tf_op args[4]
  1.7 0.0 copy-done.3
  1.8 0.0 copy-done.5
  1.8 0.0 copy-done.6
  1.8 0.0 copy-start
  1.8 1.0 %copy-done = bf16[8,128,256]{2,1,0:T(8,128)(2,1)S(1)} copy-done((bf16[8,128,256]{2,1,0:T(8,128)(2,1)S(1)}, bf16[8,128,256]{2,1,0:T(8,128)(2,1)}, u32[]{:S(2)}) %copy-start) | copy-done | bytes 524312
  2.8 0.0 copy-start.1
  2.8 1.0 %copy-done.1 = bf16[16,128,128]{2,1,0:T(8,128)(2,1)S(1)} copy-done((bf16[16,128,128]{2,1,0:T(8,128)(2,1)S(1)}, bf16[16,128,128]{2,1,0:T(8,128)(2,1)}, u32[]{:S(2)}) %copy-start.1) | copy-done | bytes 524312
  3.9 0.0 copy-start.2
  3.9 0.9 %copy-done.2 = bf16[1024,128]{1,0:T(8,128)(2,1)S(1)} copy-done((bf16[1024,128]{1,0:T(8,128)(2,1)S(1)}, bf16[1024,128]{1,0:T(8,128)(2,1)}, u32[]{:S(2)}) %copy-start.2) | copy-done | bytes 262168
  4.8 0.0 copy-start.4
  4.8 0.9 %copy-done.4 = bf16[512,128]{1,0:T(8,128)(2,1)S(1)} copy-done((bf16[512,128]{1,0:T(8,128)(2,1)S(1)}, bf16[512,128]{1,0:T(8,128)(2,1)}, u32[]{:S(2)}) %copy-start.4) | copy-done | bytes 131096
  5.7 73.9 %shard_map.91 = bf16[16,128,128]{2,1,0:T(8,128)(2,1)S(1)} custom-call(bf16[8,128,256]{2,1,0:T(8,128)(2,1)S(1)} %copy-done, bf16[16,128,128]{2,1,0:T(8,128)(2,1)S(1)} %copy-done.1, f32[1,256]{1,0:T(1,128)S(1)} %bitcast.2, bf16[256,32]{1,0:T(8,128)(2,1)S(1)} %copy.10.w1_ref, bf16[256,32]{1,0:T(8,128)(2,1)S(1)} %copy.11.w2_ref, ...), custom_call_target="tpu_custom_call" | custom-call | tf_op jit(solution)/shard_map/pallas_call | solution.py:434
  79.6 0.8 copy.13
Async XLA Ops:
  0.0 1.7 %copy-start.3 = (bf16[128,512]{1,0:T(8,128)(2,1)S(1)}, bf16[128,512]{1,0:T(8,128)(2,1)}, u32[]{:S(2)}) copy-start(bf16[128,512]{1,0:T(8,128)(2,1)} %wa_hbm.1) | copy-start | bytes 393220
  0.9 0.9 %copy-start.5 = (f32[256]{0:T(256)S(1)}, f32[256]{0:T(256)}, u32[]{:S(2)}) copy-start(f32[256]{0:T(256)} %param.11) | copy-start | bytes 3076
  0.9 0.9 %copy-start.6 = (f32[128]{0:T(128)S(1)}, f32[128]{0:T(128)}, u32[]{:S(2)}) copy-start(f32[128]{0:T(128)} %param.15) | copy-start | bytes 1540
  1.8 1.0 %copy-start = (bf16[8,128,256]{2,1,0:T(8,128)(2,1)S(1)}, bf16[8,128,256]{2,1,0:T(8,128)(2,1)}, u32[]{:S(2)}) copy-start(bf16[8,128,256]{2,1,0:T(8,128)(2,1)} %x_ref.1) | copy-start | bytes 1572868
  2.8 1.0 %copy-start.1 = (bf16[16,128,128]{2,1,0:T(8,128)(2,1)S(1)}, bf16[16,128,128]{2,1,0:T(8,128)(2,1)}, u32[]{:S(2)}) copy-start(bf16[16,128,128]{2,1,0:T(8,128)(2,1)} %cpl_hbm.1) | copy-start | bytes 1572868
  3.9 0.9 %copy-start.2 = (bf16[1024,128]{1,0:T(8,128)(2,1)S(1)}, bf16[1024,128]{1,0:T(8,128)(2,1)}, u32[]{:S(2)}) copy-start(bf16[1024,128]{1,0:T(8,128)(2,1)} %w3_hbm.1) | copy-start | bytes 786436
  4.8 0.9 %copy-start.4 = (bf16[512,128]{1,0:T(8,128)(2,1)S(1)}, bf16[512,128]{1,0:T(8,128)(2,1)}, u32[]{:S(2)}) copy-start(bf16[512,128]{1,0:T(8,128)(2,1)} %wb_hbm.1) | copy-start | bytes 393220

commit v2 on v1

v2 whole, which is shorter than its diff:
```python
import jax
import jax.numpy as jnp
from jax import lax
from jax.experimental import pallas as pl
from jax.experimental.pallas import tpu as pltpu
from jax.sharding import PartitionSpec as P

MESH = pl.DeviceIdType.MESH
F32 = jnp.float32
BF16 = jnp.bfloat16
EPS = 1e-5


def kernel(
    x_hbm,
    cpl_hbm,
    g1_hbm,
    w1_hbm,
    w2_hbm,
    w3_hbm,
    g2_hbm,
    wa_hbm,
    wb_hbm,
    out_ref,
    x_ref,
    cpl_ref,
    g1_ref,
    w1_ref,
    w2_ref,
    w3_ref,
    g2_ref,
    wa_ref,
    wb_ref,
    w3f_ref,
    wt_ref,
    xn_ref,
    tf_ref,
    lx_ref,
    rx_ref,
    xl_ref,
    xr_ref,
    lz_ref,
    lb_ref,
    lt_ref,
    rb_ref,
    oall_ref,
    in_sem,
    xsend,
    xrecv,
    rsend,
    rrecv,
    sibsend,
    sibrecv,
    zsend,
    zrecv,
    psend,
    precv,
):
    r = lax.axis_index("rows")
    zl = lax.axis_index("cols")
    core = r % 2
    zh = (r // 2) % 2
    y = (r // 4) % 4
    x = r // 16
    z = zh * 8 + zl

    loads = [
        pltpu.make_async_copy(src, dst, in_sem.at[n])
        for n, (src, dst) in enumerate(
            [
                (x_hbm, x_ref),
                (g1_hbm, g1_ref),
                (w1_hbm, w1_ref),
                (w2_hbm, w2_ref),
                (w3_hbm, w3_ref),
                (cpl_hbm, cpl_ref),
                (g2_hbm, g2_ref),
                (wa_hbm, wa_ref),
                (wb_hbm, wb_ref),
            ]
        )
    ]
    for load in loads:
        load.start()

    def rows_of(xx, yy, hh, kk):
        return ((xx * 4 + yy) * 2 + hh) * 2 + kk

    sib = (rows_of(x, y, zh, 1 - core), zl)

    def zdev(dz):
        zz = (z + dz + 16) % 16
        return (rows_of(x, y, zz // 8, core), zz % 8)

    barrier = pltpu.get_barrier_semaphore()
    pl.semaphore_signal(barrier, inc=1, device_id=sib, device_id_type=MESH)
    for dz in (8, 1, -1):
        pl.semaphore_signal(barrier, inc=1, device_id=zdev(dz), device_id_type=MESH)

    def greet_plane(d, _):
        px = (x + d // 4) % 4
        py = (y + d % 4) % 4
        pl.semaphore_signal(
            barrier, inc=1, device_id=(rows_of(px, py, zh, core), zl), device_id_type=MESH
        )
        return 0

    lax.fori_loop(1, 16, greet_plane, 0)

    for load in loads[:4]:
        load.wait()
    gain = g1_ref[...]
    for s in range(8):
        xs = x_ref[s].astype(F32)
        mean = jnp.mean(xs, axis=-1, keepdims=True)
        cen = xs - mean
        var = jnp.mean(cen * cen, axis=-1, keepdims=True)
        xn_ref[s * 128 : (s + 1) * 128, :] = (cen * lax.rsqrt(var + EPS) * gain).astype(BF16)
    wcat = jnp.concatenate([w1_ref[...]] * 4 + [w2_ref[...]] * 4, axis=0)
    for s in range(8):
        both = lax.dot_general(
            xn_ref[s * 128 : (s + 1) * 128, :],
            wcat,
            (((1,), (1,)), ((), ())),
            preferred_element_type=F32,
        )
        tf_ref[pl.ds(s, 128, stride=8), :] = both[:, :128]
        right = both[:, 128:].T
        rx_ref[pl.ds(s, 32, stride=8), :] = right[:32]
    lane = lax.broadcasted_iota(jnp.int32, (8, 128), 1) // 32
    for kk in range(2):
        for hh in range(2):
            for yy in range(2):
                gg = yy * 4 + hh * 2 + kk
                for g in range(4):
                    base = (gg * 16 + g * 4) * 8
                    tile = tf_ref[base : base + 8, :]
                    for e in range(1, 4):
                        other = tf_ref[base + e * 8 : base + e * 8 + 8, :]
                        tile = jnp.where(lane == e, other, tile)
                    lx_ref[kk, hh * 2 + yy, :, g * 128 : (g + 1) * 128] = tile

    loads[4].wait()
    for p in range(32):
        w3f_ref[pl.ds(p, 32, stride=32), :] = w3_ref[p * 32 : (p + 1) * 32, :].astype(F32)
    for n in range(8):
        wt_ref[:, n * 128 : (n + 1) * 128] = w3f_ref[n * 128 : (n + 1) * 128, :].T.astype(BF16)

    pl.semaphore_wait(barrier, 19)

    def swap(n):
        if n == 0:
            src, dst = rx_ref.at[pl.ds(pl.multiple_of((1 - core) * 128, 128), 128)], xr_ref.at[core]
        else:
            src, dst = lx_ref.at[1 - core], xl_ref.at[core]
        return pltpu.make_async_remote_copy(
            src_ref=src,
            dst_ref=dst,
            send_sem=xsend.at[n],
            recv_sem=xrecv.at[n],
            device_id=sib,
            device_id_type=MESH,
        )

    def swap_in(n):
        dst = xr_ref.at[1 - core] if n == 0 else xl_ref.at[1 - core]
        return pltpu.make_async_remote_copy(
            src_ref=dst,
            dst_ref=dst,
            send_sem=xsend.at[n],
            recv_sem=xrecv.at[n],
            device_id=sib,
            device_id_type=MESH,
        )

    swap(1).start()
    swap(0).start()
    xr_ref[core] = rx_ref[pl.ds(pl.multiple_of(core * 128, 128), 128), :]
    xl_ref[core] = lx_ref[core]

    def zcopy(up, origin, part, sem):
        return pltpu.make_async_remote_copy(
            src_ref=lz_ref.at[origin, part],
            dst_ref=lz_ref.at[origin, part],
            send_sem=zsend.at[up, sem, part],
            recv_sem=zrecv.at[origin, part],
            device_id=zdev(1 if up == 0 else -1),
            device_id_type=MESH,
        )

    def chain(up, d):
        if up == 0:
            nxt = (z + 1) % 16
            return (z - d + 16) % 16, nxt // 8, d < nxt % 8
        nxt = (z + 15) % 16
        return (z + d) % 16, nxt // 8, d < 6 - nxt % 8

    def zforward(up, d, act):
        origin, part, both = chain(up, d)
        act(zcopy(up, origin, part, d))

        @pl.when(both)
        def _():
            act(zcopy(up, origin, 1 - part, d))

    def zarrive(up, d):
        origin = chain(up, d)[0]
        zcopy(up, origin, zh, 0).wait_recv()
        other = (d - 1 < zl) if up == 0 else (d - 1 < 6 - zl)

        @pl.when(other)
        def _():
            zcopy(up, origin, 1 - zh, 0).wait_recv()

    def pcopy(origin, py2):
        cc = origin % 8
        return pltpu.make_async_remote_copy(
            src_ref=lz_ref.at[origin, zh, py2],
            dst_ref=lb_ref.at[(origin // 8) * 16 + x * 4 + y],
            send_sem=psend.at[0],
            recv_sem=precv.at[(origin // 8) * 16 + x * 4 + y],
            device_id=(rows_of(cc // 2, (cc % 2) * 2 + py2, zh, core), zl),
            device_id_type=MESH,
        )

    def spread(origin):
        cc = origin % 8

        def body(py2, _):
            here = jnp.logical_and(cc // 2 == x, (cc % 2) * 2 + py2 == y)

            @pl.when(here)
            def _():
                lb_ref[(origin // 8) * 16 + x * 4 + y] = lz_ref[origin, zh, py2]

            @pl.when(jnp.logical_not(here))
            def _():
                pcopy(origin, py2).start()

            return 0

        lax.fori_loop(0, 2, body, 0)

    def start(copy):
        copy.start()

    def sent(copy):
        copy.wait_send()

    swap_in(1).wait_recv()
    for hy in range(4):
        for g in range(4):
            cols = slice(g * 128, (g + 1) * 128)
            lz_ref[z, hy // 2, hy % 2, :, cols] = jnp.concatenate(
                [xl_ref[0, hy, :, cols], xl_ref[1, hy, :, cols]], axis=0
            ).astype(BF16)
    zforward(0, 0, start)
    zforward(1, 0, start)

    mine = zh * 16 + x * 4 + y
    swap_in(0).wait_recv()
    for q in range(16):
        rb_ref[core, mine, :, q * 128 : (q + 1) * 128] = jnp.concatenate(
            [xr_ref[0, q * 8 : (q + 1) * 8, :], xr_ref[1, q * 8 : (q + 1) * 8, :]], axis=0
        ).astype(BF16)

    def at(da, db):
        px = (x + da * (1 - core) + db * core + 4) % 4
        py = (y + da * core + db * (1 - core) + 4) % 4
        return px, py

    def slot_of(da, db, hh):
        px, py = at(da, db)
        return hh * 16 + px * 4 + py

    def dev_of(da, db):
        px, py = at(da, db)
        return (rows_of(px, py, zh, core), zl)

    zpart = zdev(8)

    def rfull(slot, dev):
        return pltpu.make_async_remote_copy(
            src_ref=rb_ref.at[core, slot],
            dst_ref=rb_ref.at[core, slot],
            send_sem=rsend.at[0],
            recv_sem=rrecv.at[slot, 0],
            device_id=dev,
            device_id_type=MESH,
        )

    def rhalf(slot, part, dev):
        piece = rb_ref.at[core, slot, :, pl.ds(part * 1024, 1024)]
        return pltpu.make_async_remote_copy(
            src_ref=piece,
            dst_ref=piece,
            send_sem=rsend.at[0],
            recv_sem=rrecv.at[slot, part],
            device_id=dev,
            device_id_type=MESH,
        )

    def scopy(slot):
        return pltpu.make_async_remote_copy(
            src_ref=rb_ref.at[core, slot],
            dst_ref=rb_ref.at[core, slot],
            send_sem=sibsend.at[0],
            recv_sem=sibrecv.at[0],
            device_id=sib,
            device_id_type=MESH,
        )

    steps = (0, -1, 1, 2)

    def begin(hh):
        slot = slot_of(0, 0, hh)
        for da, db in ((1, 0), (-1, 0), (0, 1), (0, -1)):
            rfull(slot, dev_of(da, db)).start()
        scopy(slot).start()

    def to_b(slot):
        rfull(slot, dev_of(0, 1)).start()
        rfull(slot, dev_of(0, -1)).start()
        scopy(slot).start()

    def ring_a(hh):
        for part in range(2):
            step = 1 - 2 * part
            slot = slot_of(-step, 0, hh)
            rfull(slot, dev_of(step, 0)).wait_recv()
            rhalf(slot, part, dev_of(step, 0)).start()
            to_b(slot)

    def ring_a_far(hh):
        slot = slot_of(2, 0, hh)
        for part in range(2):
            rhalf(slot, part, dev_of(1, 0)).wait_recv()
        to_b(slot)

    def ring_b(hh, n):
        for part in range(2):
            step = 1 - 2 * part
            slot = slot_of(steps[n], -step, hh)
            rfull(slot, dev_of(0, step)).wait_recv()
            rhalf(slot, part, dev_of(0, step)).start()
            scopy(slot).start()

    def ring_b_far(hh, n):
        slot = slot_of(steps[n], 2, hh)
        for part in range(2):
            rhalf(slot, part, dev_of(0, 1)).wait_recv()
        scopy(slot).start()

    begin(zh)
    rfull(mine, zpart).start()
    spread(z)

    def zstep(d):
        zarrive(0, d)
        if d < 8:
            zforward(0, d, start)
            zarrive(1, d)
            if d < 7:
                zforward(1, d, start)
        spread(chain(0, d)[0])
        if d < 8:
            spread(chain(1, d)[0])

    other = 1 - zh
    zstep(1)
    ring_a(zh)
    zstep(2)
    ring_b(zh, 0)
    ring_a_far(zh)
    zstep(3)
    rfull(slot_of(0, 0, other), zpart).wait_recv()
    begin(other)
    ring_b(zh, 1)
    ring_b(zh, 2)
    zstep(4)
    ring_a(other)
    ring_b(zh, 3)
    zstep(5)
    ring_b(other, 0)
    ring_a_far(other)
    zstep(6)
    ring_b(other, 1)
    ring_b(other, 2)
    zstep(7)
    ring_b(other, 3)
    zstep(8)
    for hh in (zh, other):
        for n in range(4):
            ring_b_far(hh, n)

    def pwait(slot, _):
        @pl.when(slot % 16 != x * 4 + y)
        def _():
            pltpu.make_async_remote_copy(
                src_ref=lb_ref.at[slot],
                dst_ref=lb_ref.at[slot],
                send_sem=psend.at[0],
                recv_sem=precv.at[slot],
                device_id=sib,
                device_id_type=MESH,
            ).wait_recv()

        return 0

    lax.fori_loop(0, 32, pwait, 0)
    for n in range(4):
        for m in range(4):
            lt_ref[m * 128 : (m + 1) * 128, n * 128 : (n + 1) * 128] = (
                lb_ref[n * 8 : (n + 1) * 8, :, m * 128 : (m + 1) * 128].reshape(128, 128).T
            )

    pltpu.make_async_remote_copy(
        src_ref=rb_ref.at[1 - core],
        dst_ref=rb_ref.at[1 - core],
        send_sem=sibsend.at[0],
        recv_sem=sibrecv.at[0],
        device_id=sib,
        device_id_type=MESH,
    ).wait_recv()

    for h in range(2):

        def outer(qb, _, h=h):
            off = pl.multiple_of(qb * 256, 256)
            right = rb_ref[h, :, :, pl.ds(off, 256)].reshape(512, 256)
            prod = jnp.dot(lt_ref[...], right, preferred_element_type=F32).astype(BF16)
            row = pl.multiple_of((h * 16 + qb * 2) * 32, 64)
            for i in range(16):
                for q in range(2):
                    oall_ref[
                        i // 2, pl.ds(row + q * 32, 32), (i % 2) * 128 : (i % 2 + 1) * 128
                    ] = prod[i * 32 : (i + 1) * 32, q * 128 : (q + 1) * 128]
            return 0

        lax.fori_loop(0, 8, outer, 0)

    for load in loads[5:]:
        load.wait()
    gain2 = g2_ref[...]

    def finish(n, _):
        for m in range(2):
            up = jnp.dot(wt_ref[...], oall_ref[n * 2 + m], preferred_element_type=F32)
            mids = []
            for k in range(2):
                i = n * 4 + m * 2 + k
                mids.append(
                    cpl_ref[i].astype(F32) + up[:, k * 128 : (k + 1) * 128].T * (1.0 / 512.0)
                )
            mid = jnp.concatenate(mids, axis=0)
            mean = jnp.mean(mid, axis=-1, keepdims=True)
            cen = mid - mean
            var = jnp.mean(cen * cen, axis=-1, keepdims=True)
            normed = (cen * lax.rsqrt(var + EPS) * gain2).astype(BF16)
            hidden = jnp.maximum(
                jnp.dot(normed, wa_ref[...], preferred_element_type=F32), 0.0
            ).astype(BF16)
            res = mid + jnp.dot(hidden, wb_ref[...], preferred_element_type=F32)
            out_ref[pl.ds(n * 4 + m * 2, 2)] = res.astype(BF16).reshape(2, 128, 128)
        return 0

    lax.fori_loop(0, 4, finish, 0)

    swap(0).wait_send()
    swap(1).wait_send()
    for ref, sem in (
        (rb_ref.at[core, pl.ds(0, 31)], rsend),
        (rb_ref.at[core], sibsend),
        (lb_ref.at[pl.ds(0, 30)], psend),
    ):
        pltpu.make_async_remote_copy(
            src_ref=ref,
            dst_ref=ref,
            send_sem=sem.at[0],
            recv_sem=sibrecv.at[0],
            device_id=sib,
            device_id_type=MESH,
        ).wait_send()
    for d in range(8):
        zforward(0, d, sent)
        if d < 7:
            zforward(1, d, sent)


def on_device(x, cpl, g1, w1, w2, w3, g2, wa, wb):
    vmem = pl.BlockSpec(memory_space=pltpu.VMEM)
    hbm = pl.BlockSpec(memory_space=pl.ANY)
    dma = pltpu.SemaphoreType.DMA
    args = (x, cpl, g1.reshape(1, 256), w1.T, w2.T, w3, g2.reshape(1, 128), wa, wb)
    return pl.pallas_call(
        kernel,
        out_shape=jax.ShapeDtypeStruct(cpl.shape, BF16),
        in_specs=[hbm] * len(args),
        out_specs=vmem,
        scratch_shapes=[pltpu.VMEM(a.shape, a.dtype) for a in args]
        + [
            pltpu.VMEM((1024, 128), F32),
            pltpu.VMEM((128, 1024), BF16),
            pltpu.VMEM((1024, 256), BF16),
            pltpu.VMEM((1024, 128), F32),
            pltpu.VMEM((2, 4, 8, 512), F32),
            pltpu.VMEM((256, 128), F32),
            pltpu.VMEM((2, 4, 8, 512), F32),
            pltpu.VMEM((2, 128, 128), F32),
            pltpu.VMEM((16, 2, 2, 16, 512), BF16),
            pltpu.VMEM((32, 16, 512), BF16),
            pltpu.VMEM((512, 512), BF16),
            pltpu.VMEM((2, 32, 16, 2048), BF16),
            pltpu.VMEM((8, 1024, 256), BF16),
            dma((len(args),)),
            dma((2,)),
            dma((2,)),
            dma((1,)),
            dma((32, 2)),
            dma((1,)),
            dma((1,)),
            dma((2, 8, 2)),
            dma((16, 2)),
            dma((1,)),
            dma((32,)),
        ],
        compiler_params=pltpu.CompilerParams(
            collective_id=0, has_side_effects=True, vmem_limit_bytes=66000000
        ),
    )(*args)


def solution(mesh):
    return jax.shard_map(
        on_device,
        mesh=mesh,
        in_specs=(
            P("rows", "cols", None),
            P("rows", "cols", None),
            P(),
            P(),
            P(),
            P(),
            P(),
            P(),
            P(),
        ),
        out_specs=P("rows", "cols", None),
        check_vma=False,
    )
```

time: 80.7 us -> 68.2 us (0.85)
  Pallas kernels: 73.9 us -> 65.2 us
  local copies, waits for them, and re-layouts: 6.46 us -> 1.89 us
    pallas_call x1, Pallas kernels: 73.9 us -> 65.2 us  [on_device(): pl.pallas_call(kernel, out_shape=jax.ShapeDtypeStruct(cpl.shape, BF16), i...]
    unnamed x17 -> x1, local copies, waits for them, and re-layouts: 6.46 us -> 1.89 us
where the time goes in v2:
time: 68.2 us; the launch traced here: 67.1 us
  Pallas kernels  65.2 us (96%)
  local copies, waits for them, and re-layouts  1.89 us (3%)
    pallas_call x1, Pallas kernels, on_device(): pl.pallas_call(kernel, out_shape=jax.ShapeDtypeStruct(cpl.shape, BF16), i...  65.2 us
    unnamed x1, local copies, waits for them, and re-layouts  1.89 us

profile of v2, /device:TPU:1, one launch (start us, length us, event | category | flops | bytes accessed | tf_op | source)
XLA Modules:
  0.0 67.1 jit_solution(4460332951650672842)
XLA Ops:
  0.0 65.2 %shard_map.91 = bf16[16,128,128]{2,1,0:T(8,128)(2,1)} custom-call(bf16[8,128,256]{2,1,0:T(8,128)(2,1)} %x_hbm.1, bf16[16,128,128]{2,1,0:T(8,128)(2,1)} %cpl_hbm.1, f32[1,256]{1,0:T(1,128)} %bitcast.6, bf16[32,256]{1,0:T(8,128)(2,1)} %bitcast.4, bf16[32,256]{1,0:T(8,128)(2,1)} %bitcast.5, bf16[1024,128]{1,0:T(8,128)(2,1)} %w3_hbm.1, f32[1,128]{1,0:T(1,128)} %bitcast.7, ...), custom_call_target="tpu_custom_call" | custom-call | tf_op jit(solution)/shard_map/pallas_call | solution.py:495
  65.2 1.9 %copy.11 = bf16[16,128,128]{2,1,0:T(8,128)(2,1)} copy(bf16[16,128,128]{2,1,0:T(8,128)(2,1)} %shard_map.91) | data formatting | bytes 1048576

commit v3 on v2

v3 whole, which is shorter than its diff:
```python
import jax
import jax.numpy as jnp
from jax import lax
from jax.experimental import pallas as pl
from jax.experimental.pallas import tpu as pltpu
from jax.sharding import PartitionSpec as P

MESH = pl.DeviceIdType.MESH
F32 = jnp.float32
BF16 = jnp.bfloat16
EPS = 1e-5


def kernel(
    x_hbm,
    cpl_hbm,
    g1_hbm,
    w1_hbm,
    w2_hbm,
    w3_hbm,
    g2_hbm,
    wa_hbm,
    wb_hbm,
    out_hbm,
    x_ref,
    cpl_ref,
    g1_ref,
    w1_ref,
    w2_ref,
    w3_ref,
    g2_ref,
    wa_ref,
    wb_ref,
    w3f_ref,
    wt_ref,
    xn_ref,
    tf_ref,
    lx_ref,
    rx_ref,
    xl_ref,
    xr_ref,
    lz_ref,
    lb_ref,
    lt_ref,
    rb_ref,
    ry_ref,
    oall_ref,
    mid_ref,
    nrm_ref,
    res_ref,
    in_sem,
    out_sem,
    xsend,
    xrecv,
    rsend,
    rrecv,
    sibsend,
    sibrecv,
    rysend,
    ryrecv,
    zsend,
    zrecv,
    psend,
    precv,
):
    r = lax.axis_index("rows")
    zl = lax.axis_index("cols")
    core = r % 2
    zh = (r // 2) % 2
    y = (r // 4) % 4
    x = r // 16
    z = zh * 8 + zl

    loads = [
        pltpu.make_async_copy(src, dst, in_sem.at[n])
        for n, (src, dst) in enumerate(
            [
                (x_hbm, x_ref),
                (g1_hbm, g1_ref),
                (w1_hbm, w1_ref),
                (w2_hbm, w2_ref),
                (w3_hbm, w3_ref),
                (cpl_hbm, cpl_ref),
                (g2_hbm, g2_ref),
                (wa_hbm, wa_ref),
                (wb_hbm, wb_ref),
            ]
        )
    ]
    for load in loads:
        load.start()

    def rows_of(xx, yy, hh, kk):
        return ((xx * 4 + yy) * 2 + hh) * 2 + kk

    sib = (rows_of(x, y, zh, 1 - core), zl)

    def zdev(dz):
        zz = (z + dz + 16) % 16
        return (rows_of(x, y, zz // 8, core), zz % 8)

    barrier = pltpu.get_barrier_semaphore()
    pl.semaphore_signal(barrier, inc=1, device_id=sib, device_id_type=MESH)
    for dz in (1, -1, 4, -4):
        pl.semaphore_signal(barrier, inc=1, device_id=zdev(dz), device_id_type=MESH)

    def greet_plane(d, _):
        px = (x + d // 4) % 4
        py = (y + d % 4) % 4
        pl.semaphore_signal(
            barrier, inc=1, device_id=(rows_of(px, py, zh, core), zl), device_id_type=MESH
        )
        return 0

    lax.fori_loop(1, 16, greet_plane, 0)

    for load in loads[:4]:
        load.wait()
    gain = g1_ref[...]
    for s in range(8):
        xs = x_ref[s].astype(F32)
        mean = jnp.mean(xs, axis=-1, keepdims=True)
        cen = xs - mean
        var = jnp.mean(cen * cen, axis=-1, keepdims=True)
        xn_ref[s * 128 : (s + 1) * 128, :] = (cen * lax.rsqrt(var + EPS) * gain).astype(BF16)
    wcat = jnp.concatenate([w1_ref[...]] * 4 + [w2_ref[...]] * 4, axis=0)
    for s in range(8):
        both = lax.dot_general(
            xn_ref[s * 128 : (s + 1) * 128, :],
            wcat,
            (((1,), (1,)), ((), ())),
            preferred_element_type=F32,
        )
        tf_ref[pl.ds(s, 128, stride=8), :] = both[:, :128]
        right = both[:, 128:].T
        rx_ref[pl.ds(s, 32, stride=8), :] = right[:32]
    lane = lax.broadcasted_iota(jnp.int32, (8, 128), 1) // 32
    for kk in range(2):
        for hh in range(2):
            for yy in range(2):
                gg = yy * 4 + hh * 2 + kk
                for g in range(4):
                    base = (gg * 16 + g * 4) * 8
                    tile = tf_ref[base : base + 8, :]
                    for e in range(1, 4):
                        other = tf_ref[base + e * 8 : base + e * 8 + 8, :]
                        tile = jnp.where(lane == e, other, tile)
                    lx_ref[kk, hh * 2 + yy, :, g * 128 : (g + 1) * 128] = tile

    pl.semaphore_wait(barrier, 20)

    def swap(n):
        if n == 0:
            src, dst = rx_ref.at[pl.ds(pl.multiple_of((1 - core) * 128, 128), 128)], xr_ref.at[core]
        else:
            src, dst = lx_ref.at[1 - core], xl_ref.at[core]
        return pltpu.make_async_remote_copy(
            src_ref=src,
            dst_ref=dst,
            send_sem=xsend.at[n],
            recv_sem=xrecv.at[n],
            device_id=sib,
            device_id_type=MESH,
        )

    def swap_in(n):
        dst = xr_ref.at[1 - core] if n == 0 else xl_ref.at[1 - core]
        return pltpu.make_async_remote_copy(
            src_ref=dst,
            dst_ref=dst,
            send_sem=xsend.at[n],
            recv_sem=xrecv.at[n],
            device_id=sib,
            device_id_type=MESH,
        )

    swap(0).start()
    swap(1).start()
    xr_ref[core] = rx_ref[pl.ds(pl.multiple_of(core * 128, 128), 128), :]
    xl_ref[core] = lx_ref[core]

    def zmessage(way, d):
        last = 8 - way
        return (last,) if d < last else ()

    def half_of(zz):
        return ((zz + 32) % 16) // 8

    def zparts(way, origin, d):
        sgn = 1 - 2 * way
        part = half_of(origin + sgn * d)
        count = 0
        for e in zmessage(way, d):
            count = count + (half_of(origin + sgn * e) + part) % 2
        return part, count

    def zcopy(way, origin, part, d, hop):
        return pltpu.make_async_remote_copy(
            src_ref=lz_ref.at[origin, part],
            dst_ref=lz_ref.at[origin, part],
            send_sem=zsend.at[way, d, part],
            recv_sem=zrecv.at[origin, part],
            device_id=zdev(hop),
            device_id_type=MESH,
        )

    zfrom = {d: (d - 1, 1) for d in range(1, 9)}

    def zput(way, d, act):
        at_d, hop = zfrom[d]
        sgn = 1 - 2 * way
        origin = (z - sgn * at_d + 16) % 16
        part, count = zparts(way, origin, d)
        act(zcopy(way, origin, part, d, sgn * hop))
        if zmessage(way, d):

            @pl.when(count > 0)
            def _():
                act(zcopy(way, origin, 1 - part, d, sgn * hop))

    def zget(way, d):
        sgn = 1 - 2 * way
        origin = (z - sgn * d + 16) % 16
        part, count = zparts(way, origin, d)
        zcopy(way, origin, zh, d, 1).wait_recv()
        if zmessage(way, d):

            @pl.when(count > 0)
            def _():
                zcopy(way, origin, 1 - zh, d, 1).wait_recv()

        return origin

    def pcopy(origin, py2):
        cc = origin % 8
        return pltpu.make_async_remote_copy(
            src_ref=lz_ref.at[origin, zh, py2],
            dst_ref=lb_ref.at[(origin // 8) * 16 + x * 4 + y],
            send_sem=psend.at[0],
            recv_sem=precv.at[(origin // 8) * 16 + x * 4 + y],
            device_id=(rows_of(cc // 2, (cc % 2) * 2 + py2, zh, core), zl),
            device_id_type=MESH,
        )

    def spread(origin):
        cc = origin % 8

        def body(py2, _):
            here = jnp.logical_and(cc // 2 == x, (cc % 2) * 2 + py2 == y)

            @pl.when(here)
            def _():
                lb_ref[(origin // 8) * 16 + x * 4 + y] = lz_ref[origin, zh, py2]

            @pl.when(jnp.logical_not(here))
            def _():
                pcopy(origin, py2).start()

            return 0

        lax.fori_loop(0, 2, body, 0)

    def start(copy):
        copy.start()

    def sent(copy):
        copy.wait_send()

    mine = zh * 16 + x * 4 + y
    swap_in(0).wait_recv()
    for q in range(16):
        rb_ref[core, mine, :, q * 128 : (q + 1) * 128] = jnp.concatenate(
            [xr_ref[0, q * 8 : (q + 1) * 8, :], xr_ref[1, q * 8 : (q + 1) * 8, :]], axis=0
        ).astype(BF16)

    def at(da, db):
        px = (x + da * (1 - core) + db * core + 4) % 4
        py = (y + da * core + db * (1 - core) + 4) % 4
        return px, py

    def slot_of(da, db, hh):
        px, py = at(da, db)
        return hh * 16 + px * 4 + py

    def dev_of(da, db):
        px, py = at(da, db)
        return (rows_of(px, py, zh, core), zl)

    def rfull(slot, dev):
        return pltpu.make_async_remote_copy(
            src_ref=rb_ref.at[core, slot],
            dst_ref=rb_ref.at[core, slot],
            send_sem=rsend.at[0],
            recv_sem=rrecv.at[slot, 0],
            device_id=dev,
            device_id_type=MESH,
        )

    def rhalf(slot, part, dev):
        piece = rb_ref.at[core, slot, :, pl.ds(part * 1024, 1024)]
        return pltpu.make_async_remote_copy(
            src_ref=piece,
            dst_ref=piece,
            send_sem=rsend.at[0],
            recv_sem=rrecv.at[slot, part],
            device_id=dev,
            device_id_type=MESH,
        )

    def scopy(slot):
        return pltpu.make_async_remote_copy(
            src_ref=rb_ref.at[core, slot],
            dst_ref=rb_ref.at[core, slot],
            send_sem=sibsend.at[0],
            recv_sem=sibrecv.at[0],
            device_id=sib,
            device_id_type=MESH,
        )

    steps = (0, -1, 1, 2)

    def begin(hh):
        slot = slot_of(0, 0, hh)
        for da, db in ((1, 0), (-1, 0), (0, 1), (0, -1)):
            rfull(slot, dev_of(da, db)).start()
        scopy(slot).start()

    def to_b(slot):
        rfull(slot, dev_of(0, 1)).start()
        rfull(slot, dev_of(0, -1)).start()
        scopy(slot).start()

    def ring_a(hh):
        for part in range(2):
            step = 1 - 2 * part
            slot = slot_of(-step, 0, hh)
            rfull(slot, dev_of(step, 0)).wait_recv()
            rhalf(slot, part, dev_of(step, 0)).start()
            to_b(slot)

    def ring_a_far(hh):
        slot = slot_of(2, 0, hh)
        for part in range(2):
            rhalf(slot, part, dev_of(1, 0)).wait_recv()
        to_b(slot)

    def ring_b(hh, n):
        for part in range(2):
            step = 1 - 2 * part
            slot = slot_of(steps[n], -step, hh)
            rfull(slot, dev_of(0, step)).wait_recv()
            rhalf(slot, part, dev_of(0, step)).start()
            scopy(slot).start()

    def ring_b_far(hh, n):
        slot = slot_of(steps[n], 2, hh)
        for part in range(2):
            rhalf(slot, part, dev_of(0, 1)).wait_recv()
        scopy(slot).start()

    def begin_straight(hh):
        slot = slot_of(0, 0, hh)
        for step in (1, -1, 2):
            rfull(slot, dev_of(step, 0)).start()
        for step in (1, -1, 2):
            rfull(slot, dev_of(0, step)).start()
        scopy(slot).start()

    def ring_a_straight(hh):
        for da in (-1, 1, 2):
            slot = slot_of(da, 0, hh)
            rfull(slot, dev_of(1, 0)).wait_recv()
            for step in (1, -1, 2):
                rfull(slot, dev_of(0, step)).start()
            scopy(slot).start()

    def ring_b_straight(hh, n):
        for db in (-1, 1, 2):
            slot = slot_of(steps[n], db, hh)
            rfull(slot, dev_of(0, 1)).wait_recv()
            scopy(slot).start()

    theirs = slot_of(0, 0, 1 - zh)

    def rout(part):
        return pltpu.make_async_remote_copy(
            src_ref=rb_ref.at[core, mine, :, pl.ds(part * 1024, 1024)],
            dst_ref=ry_ref.at[part],
            send_sem=rysend.at[part],
            recv_sem=ryrecv.at[part],
            device_id=zdev(4 - 8 * part),
            device_id_type=MESH,
        )

    def ron(part):
        slot = half_of(z - 4 + 8 * part) * 16 + x * 4 + y
        return pltpu.make_async_remote_copy(
            src_ref=ry_ref.at[part],
            dst_ref=rb_ref.at[core, slot, :, pl.ds(part * 1024, 1024)],
            send_sem=rysend.at[2 + part],
            recv_sem=rrecv.at[slot, part],
            device_id=zdev(4 - 8 * part),
            device_id_type=MESH,
        )

    rout(0).start()
    rout(1).start()
    begin(zh)
    swap_in(1).wait_recv()
    for hy in range(4):
        for g in range(4):
            cols = slice(g * 128, (g + 1) * 128)
            lz_ref[z, hy // 2, hy % 2, :, cols] = jnp.concatenate(
                [xl_ref[0, hy, :, cols], xl_ref[1, hy, :, cols]], axis=0
            ).astype(BF16)
    for way in range(2):
        zput(way, 1, start)
    spread(z)

    loads[4].wait()
    for p in range(32):
        w3f_ref[pl.ds(p, 32, stride=32), :] = w3_ref[p * 32 : (p + 1) * 32, :].astype(F32)
    for n in range(8):
        wt_ref[:, n * 128 : (n + 1) * 128] = w3f_ref[n * 128 : (n + 1) * 128, :].T.astype(BF16)

    def zstep(d):
        ways = range(1 if d == 8 else 2)
        origins = []
        for way in ways:
            origins.append(zget(way, d))
            for nxt, (at_d, _) in zfrom.items():
                if at_d == d and nxt <= 8 - way:
                    zput(way, nxt, start)
        for origin in origins:
            spread(origin)

    other = 1 - zh
    ring_a(zh)
    ring_b(zh, 0)
    for part in range(2):
        rout(part).wait_recv()
        ron(part).start()
    zstep(1)
    ring_a_far(zh)
    zstep(2)
    ring_b(zh, 1)
    ring_b(zh, 2)
    zstep(3)
    for part in range(2):
        rhalf(theirs, part, dev_of(1, 0)).wait_recv()
    begin_straight(other)
    ring_b(zh, 3)
    zstep(4)
    ring_a_straight(other)
    zstep(5)
    for n in range(4):
        ring_b_far(zh, n)
    zstep(6)
    ring_b_straight(other, 0)
    zstep(7)
    ring_b_straight(other, 1)
    zstep(8)
    ring_b_straight(other, 2)
    ring_b_straight(other, 3)

    def pwait(slot, _):
        @pl.when(slot % 16 != x * 4 + y)
        def _():
            pltpu.make_async_remote_copy(
                src_ref=lb_ref.at[slot],
                dst_ref=lb_ref.at[slot],
                send_sem=psend.at[0],
                recv_sem=precv.at[slot],
                device_id=sib,
                device_id_type=MESH,
            ).wait_recv()

        return 0

    lax.fori_loop(0, 32, pwait, 0)
    for n in range(4):
        for m in range(4):
            lt_ref[m * 128 : (m + 1) * 128, n * 128 : (n + 1) * 128] = (
                lb_ref[n * 8 : (n + 1) * 8, :, m * 128 : (m + 1) * 128].reshape(128, 128).T
            )

    pltpu.make_async_remote_copy(
        src_ref=rb_ref.at[1 - core],
        dst_ref=rb_ref.at[1 - core],
        send_sem=sibsend.at[0],
        recv_sem=sibrecv.at[0],
        device_id=sib,
        device_id_type=MESH,
    ).wait_recv()

    for h in range(2):

        def outer(qb, _, h=h):
            off = pl.multiple_of(qb * 512, 512)
            right = rb_ref[h, :, :, pl.ds(off, 512)].reshape(512, 512)
            prod = jnp.dot(lt_ref[...], right, preferred_element_type=F32).astype(BF16)
            row = pl.multiple_of((h * 16 + qb * 4) * 32, 128)
            for i in range(16):
                for q in range(4):
                    oall_ref[
                        i // 2, pl.ds(row + q * 32, 32), (i % 2) * 128 : (i % 2 + 1) * 128
                    ] = prod[i * 32 : (i + 1) * 32, q * 128 : (q + 1) * 128]
            return 0

        lax.fori_loop(0, 4, outer, 0)

    for load in loads[5:]:
        load.wait()
    gain2 = g2_ref[...]

    def contract(n, _):
        for m in range(4):
            up = jnp.dot(wt_ref[...], oall_ref[n * 4 + m], preferred_element_type=F32)
            for k in range(2):
                i = n * 8 + m * 2 + k
                mid_ref[i] = cpl_ref[i].astype(F32) + up[:, k * 128 : (k + 1) * 128].T * (
                    1.0 / 512.0
                )
        return 0

    lax.fori_loop(0, 2, contract, 0)

    def norm_pair(n, _):
        mid = mid_ref[pl.ds(n * 4, 4)].reshape(512, 128)
        mean = jnp.mean(mid, axis=-1, keepdims=True)
        cen = mid - mean
        var = jnp.mean(cen * cen, axis=-1, keepdims=True)
        nrm_ref[n] = (cen * lax.rsqrt(var + EPS) * gain2).astype(BF16)
        return 0

    lax.fori_loop(0, 4, norm_pair, 0)

    def result(n):
        return pltpu.make_async_copy(
            res_ref.at[pl.ds(n * 4, 4)], out_hbm.at[pl.ds(n * 4, 4)], out_sem.at[n]
        )

    def transition(n, _):
        hidden = jnp.maximum(
            jnp.dot(nrm_ref[n], wa_ref[...], preferred_element_type=F32), 0.0
        ).astype(BF16)
        res = mid_ref[pl.ds(n * 4, 4)].reshape(512, 128) + jnp.dot(
            hidden, wb_ref[...], preferred_element_type=F32
        )
        res_ref[pl.ds(n * 4, 4)] = res.astype(BF16).reshape(4, 128, 128)
        result(n).start()
        return 0

    lax.fori_loop(0, 4, transition, 0)

    swap(0).wait_send()
    swap(1).wait_send()
    for ref, sem in (
        (rb_ref.at[core, pl.ds(0, 30)], rsend),
        (rb_ref.at[core], sibsend),
        (lb_ref.at[pl.ds(0, 30)], psend),
    ):
        pltpu.make_async_remote_copy(
            src_ref=ref,
            dst_ref=ref,
            send_sem=sem.at[0],
            recv_sem=sibrecv.at[0],
            device_id=sib,
            device_id_type=MESH,
        ).wait_send()
    for part in range(2):
        rout(part).wait_send()
        ron(part).wait_send()
    for d in range(1, 9):
        for way in range(1 if d == 8 else 2):
            zput(way, d, sent)
    for n in range(4):
        result(n).wait()


def on_device(x, cpl, g1, w1, w2, w3, g2, wa, wb):
    hbm = pl.BlockSpec(memory_space=pltpu.HBM)
    dma = pltpu.SemaphoreType.DMA
    args = (x, cpl, g1.reshape(1, 256), w1.T, w2.T, w3, g2.reshape(1, 128), wa, wb)
    return pl.pallas_call(
        kernel,
        out_shape=jax.ShapeDtypeStruct(cpl.shape, BF16),
        in_specs=[hbm] * len(args),
        out_specs=hbm,
        scratch_shapes=[pltpu.VMEM(a.shape, a.dtype) for a in args]
        + [
            pltpu.VMEM((1024, 128), F32),
            pltpu.VMEM((128, 1024), BF16),
            pltpu.VMEM((1024, 256), BF16),
            pltpu.VMEM((1024, 128), F32),
            pltpu.VMEM((2, 4, 8, 512), F32),
            pltpu.VMEM((256, 128), F32),
            pltpu.VMEM((2, 4, 8, 512), F32),
            pltpu.VMEM((2, 128, 128), F32),
            pltpu.VMEM((16, 2, 2, 16, 512), BF16),
            pltpu.VMEM((32, 16, 512), BF16),
            pltpu.VMEM((512, 512), BF16),
            pltpu.VMEM((2, 32, 16, 2048), BF16),
            pltpu.VMEM((2, 16, 1024), BF16),
            pltpu.VMEM((8, 1024, 256), BF16),
            pltpu.VMEM((16, 128, 128), F32),
            pltpu.VMEM((4, 512, 128), BF16),
            pltpu.VMEM((16, 128, 128), BF16),
            dma((len(args),)),
            dma((4,)),
            dma((2,)),
            dma((2,)),
            dma((1,)),
            dma((32, 2)),
            dma((1,)),
            dma((1,)),
            dma((4,)),
            dma((2,)),
            dma((2, 9, 2)),
            dma((16, 2)),
            dma((1,)),
            dma((32,)),
        ],
        compiler_params=pltpu.CompilerParams(
            collective_id=0, has_side_effects=True, vmem_limit_bytes=66500000
        ),
    )(*args)


def solution(mesh):
    return jax.shard_map(
        on_device,
        mesh=mesh,
        in_specs=(
            P("rows", "cols", None),
            P("rows", "cols", None),
            P(),
            P(),
            P(),
            P(),
            P(),
            P(),
            P(),
        ),
        out_specs=P("rows", "cols", None),
        check_vma=False,
    )
```

time: 68.2 us -> 64.3 us (0.943)
  Pallas kernels: 65.2 us -> 61.8 us
    pallas_call x1, Pallas kernels: 65.2 us -> 61.8 us  [on_device(): pl.pallas_call(kernel, out_shape=jax.ShapeDtypeStruct(cpl.shape, BF16), i...]
where the time goes in v3:
time: 64.3 us; the launch traced here: 63.7 us
  Pallas kernels  61.8 us (96%)
  local copies, waits for them, and re-layouts  1.89 us (3%)
    pallas_call x1, Pallas kernels, on_device(): pl.pallas_call(kernel, out_shape=jax.ShapeDtypeStruct(cpl.shape, BF16), i...  61.8 us
    unnamed x1, local copies, waits for them, and re-layouts  1.89 us

profile of v3, /device:TPU:1, one launch (start us, length us, event | category | flops | bytes accessed | tf_op | source)
XLA Modules:
  0.0 63.7 jit_solution(4512261371906108872)
XLA Ops:
  0.0 61.8 %shard_map.91 = bf16[16,128,128]{2,1,0:T(8,128)(2,1)} custom-call(bf16[8,128,256]{2,1,0:T(8,128)(2,1)} %x_hbm.1, bf16[16,128,128]{2,1,0:T(8,128)(2,1)} %cpl_hbm.1, f32[1,256]{1,0:T(1,128)} %bitcast.6, bf16[32,256]{1,0:T(8,128)(2,1)} %bitcast.4, bf16[32,256]{1,0:T(8,128)(2,1)} %bitcast.5, bf16[1024,128]{1,0:T(8,128)(2,1)} %w3_hbm.1, f32[1,128]{1,0:T(1,128)} %bitcast.7, ...), custom_call_target="tpu_custom_call" | custom-call | tf_op jit(solution)/shard_map/pallas_call | solution.py:585
  61.8 1.9 %copy.11 = bf16[16,128,128]{2,1,0:T(8,128)(2,1)} copy(bf16[16,128,128]{2,1,0:T(8,128)(2,1)} %shard_map.91) | data formatting | bytes 1048576

commit v4 on v3

--- a/solution.py
+++ b/solution.py
@@ -195,14 +195,28 @@
         return part, count
 
     def zcopy(way, origin, part, d, hop):
-        return pltpu.make_async_remote_copy(
-            src_ref=lz_ref.at[origin, part],
-            dst_ref=lz_ref.at[origin, part],
-            send_sem=zsend.at[way, d, part],
-            recv_sem=zrecv.at[origin, part],
+        piece = lz_ref.at[origin] if part is None else lz_ref.at[origin, part]
+        return pltpu.make_async_remote_copy(
+            src_ref=piece,
+            dst_ref=piece,
+            send_sem=zsend.at[way, d],
+            recv_sem=zrecv.at[origin],
             device_id=zdev(hop),
             device_id_type=MESH,
         )
+
+    def zeither(way, origin, part, count, d, hop, act):
+        if not zmessage(way, d):
+            act(zcopy(way, origin, part, d, hop))
+            return
+
+        @pl.when(count > 0)
+        def _():
+            act(zcopy(way, origin, None, d, hop))
+
+        @pl.when(count == 0)
+        def _():
+            act(zcopy(way, origin, part, d, hop))
 
     zfrom = {d: (d - 1, 1) for d in range(1, 9)}
 
@@ -211,24 +225,13 @@
         sgn = 1 - 2 * way
         origin = (z - sgn * at_d + 16) % 16
         part, count = zparts(way, origin, d)
-        act(zcopy(way, origin, part, d, sgn * hop))
-        if zmessage(way, d):
-
-            @pl.when(count > 0)
-            def _():
-                act(zcopy(way, origin, 1 - part, d, sgn * hop))
+        zeither(way, origin, part, count, d, sgn * hop, act)
 
     def zget(way, d):
         sgn = 1 - 2 * way
         origin = (z - sgn * d + 16) % 16
         part, count = zparts(way, origin, d)
-        zcopy(way, origin, zh, d, 1).wait_recv()
-        if zmessage(way, d):
-
-            @pl.when(count > 0)
-            def _():
-                zcopy(way, origin, 1 - zh, d, 1).wait_recv()
-
+        zeither(way, origin, zh, count, d, 1, lambda copy: copy.wait_recv())
         return origin
 
     def pcopy(origin, py2):
@@ -237,7 +240,7 @@
             src_ref=lz_ref.at[origin, zh, py2],
             dst_ref=lb_ref.at[(origin // 8) * 16 + x * 4 + y],
             send_sem=psend.at[0],
-            recv_sem=precv.at[(origin // 8) * 16 + x * 4 + y],
+            recv_sem=precv.at[0],
             device_id=(rows_of(cc // 2, (cc % 2) * 2 + py2, zh, core), zl),
             device_id_type=MESH,
         )
@@ -286,23 +289,33 @@
         px, py = at(da, db)
         return (rows_of(px, py, zh, core), zl)
 
-    def rfull(slot, dev):
+    def rblocks(count, sem):
+        return pltpu.make_async_remote_copy(
+            src_ref=rb_ref.at[core, pl.ds(0, count)],
+            dst_ref=rb_ref.at[core, pl.ds(0, count)],
+            send_sem=rsend.at[0],
+            recv_sem=rrecv.at[sem],
+            device_id=sib,
+            device_id_type=MESH,
+        )
+
+    def rfull(slot, dev, sem):
         return pltpu.make_async_remote_copy(
             src_ref=rb_ref.at[core, slot],
             dst_ref=rb_ref.at[core, slot],
             send_sem=rsend.at[0],
-            recv_sem=rrecv.at[slot, 0],
+            recv_sem=rrecv.at[sem],
             device_id=dev,
             device_id_type=MESH,
         )
 
-    def rhalf(slot, part, dev):
+    def rhalf(slot, part, dev, sem):
         piece = rb_ref.at[core, slot, :, pl.ds(part * 1024, 1024)]
         return pltpu.make_async_remote_copy(
             src_ref=piece,
             dst_ref=piece,
             send_sem=rsend.at[0],
-            recv_sem=rrecv.at[slot, part],
+            recv_sem=rrecv.at[sem],
             device_id=dev,
             device_id_type=MESH,
         )
@@ -321,66 +334,61 @@
 
     def begin(hh):
         slot = slot_of(0, 0, hh)
-        for da, db in ((1, 0), (-1, 0), (0, 1), (0, -1)):
-            rfull(slot, dev_of(da, db)).start()
+        for da, db, sem in ((1, 0, 0), (-1, 0, 1), (0, 1, 3), (0, -1, 4)):
+            rfull(slot, dev_of(da, db), sem).start()
         scopy(slot).start()
 
-    def to_b(slot):
-        rfull(slot, dev_of(0, 1)).start()
-        rfull(slot, dev_of(0, -1)).start()
+    def to_b(slot, n):
+        rfull(slot, dev_of(0, 1), 3 + 2 * n).start()
+        rfull(slot, dev_of(0, -1), 4 + 2 * n).start()
         scopy(slot).start()
 
     def ring_a(hh):
         for part in range(2):
             step = 1 - 2 * part
             slot = slot_of(-step, 0, hh)
-            rfull(slot, dev_of(step, 0)).wait_recv()
-            rhalf(slot, part, dev_of(step, 0)).start()
-            to_b(slot)
+            rblocks(1, part).wait_recv()
+            rhalf(slot, part, dev_of(step, 0), 2).start()
+            to_b(slot, 1 + part)
 
     def ring_a_far(hh):
-        slot = slot_of(2, 0, hh)
-        for part in range(2):
-            rhalf(slot, part, dev_of(1, 0)).wait_recv()
-        to_b(slot)
+        rblocks(1, 2).wait_recv()
+        to_b(slot_of(2, 0, hh), 3)
 
     def ring_b(hh, n):
         for part in range(2):
             step = 1 - 2 * part
             slot = slot_of(steps[n], -step, hh)
-            rfull(slot, dev_of(0, step)).wait_recv()
-            rhalf(slot, part, dev_of(0, step)).start()
+            rblocks(1, 3 + 2 * n + part).wait_recv()
+            rhalf(slot, part, dev_of(0, step), 11).start()
             scopy(slot).start()
 
-    def ring_b_far(hh, n):
-        slot = slot_of(steps[n], 2, hh)
-        for part in range(2):
-            rhalf(slot, part, dev_of(0, 1)).wait_recv()
-        scopy(slot).start()
+    def ring_b_far(hh):
+        rblocks(4, 11).wait_recv()
+        for n in range(4):
+            scopy(slot_of(steps[n], 2, hh)).start()
 
     def begin_straight(hh):
         slot = slot_of(0, 0, hh)
+        for step, sem in ((1, 13), (-1, 14), (2, 15)):
+            rfull(slot, dev_of(step, 0), sem).start()
         for step in (1, -1, 2):
-            rfull(slot, dev_of(step, 0)).start()
-        for step in (1, -1, 2):
-            rfull(slot, dev_of(0, step)).start()
+            rfull(slot, dev_of(0, step), 16).start()
         scopy(slot).start()
 
     def ring_a_straight(hh):
-        for da in (-1, 1, 2):
-            slot = slot_of(da, 0, hh)
-            rfull(slot, dev_of(1, 0)).wait_recv()
+        for n in range(1, 4):
+            slot = slot_of(steps[n], 0, hh)
+            rblocks(1, 12 + n).wait_recv()
             for step in (1, -1, 2):
-                rfull(slot, dev_of(0, step)).start()
+                rfull(slot, dev_of(0, step), 16 + n).start()
             scopy(slot).start()
 
     def ring_b_straight(hh, n):
+        rblocks(3, 16 + n).wait_recv()
         for db in (-1, 1, 2):
-            slot = slot_of(steps[n], db, hh)
-            rfull(slot, dev_of(0, 1)).wait_recv()
-            scopy(slot).start()
-
-    theirs = slot_of(0, 0, 1 - zh)
+            scopy(slot_of(steps[n], db, hh)).start()
+
 
     def rout(part):
         return pltpu.make_async_remote_copy(
@@ -398,7 +406,7 @@
             src_ref=ry_ref.at[part],
             dst_ref=rb_ref.at[core, slot, :, pl.ds(part * 1024, 1024)],
             send_sem=rysend.at[2 + part],
-            recv_sem=rrecv.at[slot, part],
+            recv_sem=rrecv.at[12],
             device_id=zdev(4 - 8 * part),
             device_id_type=MESH,
         )
@@ -446,15 +454,13 @@
     ring_b(zh, 1)
     ring_b(zh, 2)
     zstep(3)
-    for part in range(2):
-        rhalf(theirs, part, dev_of(1, 0)).wait_recv()
+    rblocks(1, 12).wait_recv()
     begin_straight(other)
     ring_b(zh, 3)
     zstep(4)
     ring_a_straight(other)
     zstep(5)
-    for n in range(4):
-        ring_b_far(zh, n)
+    ring_b_far(zh)
     zstep(6)
     ring_b_straight(other, 0)
     zstep(7)
@@ -463,21 +469,14 @@
     ring_b_straight(other, 2)
     ring_b_straight(other, 3)
 
-    def pwait(slot, _):
-        @pl.when(slot % 16 != x * 4 + y)
-        def _():
-            pltpu.make_async_remote_copy(
-                src_ref=lb_ref.at[slot],
-                dst_ref=lb_ref.at[slot],
-                send_sem=psend.at[0],
-                recv_sem=precv.at[slot],
-                device_id=sib,
-                device_id_type=MESH,
-            ).wait_recv()
-
-        return 0
-
-    lax.fori_loop(0, 32, pwait, 0)
+    pltpu.make_async_remote_copy(
+        src_ref=lb_ref.at[pl.ds(0, 30)],
+        dst_ref=lb_ref.at[pl.ds(0, 30)],
+        send_sem=psend.at[0],
+        recv_sem=precv.at[0],
+        device_id=sib,
+        device_id_type=MESH,
+    ).wait_recv()
     for n in range(4):
         for m in range(4):
             lt_ref[m * 128 : (m + 1) * 128, n * 128 : (n + 1) * 128] = (
@@ -611,15 +610,15 @@
             dma((2,)),
             dma((2,)),
             dma((1,)),
-            dma((32, 2)),
+            dma((20,)),
             dma((1,)),
             dma((1,)),
             dma((4,)),
             dma((2,)),
-            dma((2, 9, 2)),
-            dma((16, 2)),
+            dma((2, 9)),
+            dma((16,)),
             dma((1,)),
-            dma((32,)),
+            dma((1,)),
         ],
         compiler_params=pltpu.CompilerParams(
             collective_id=0, has_side_effects=True, vmem_limit_bytes=66500000

time: 64.3 us -> 63.3 us (0.984)
  Pallas kernels: 61.8 us -> 60.8 us
    pallas_call x1, Pallas kernels: 61.8 us -> 60.8 us  [on_device(): pl.pallas_call(kernel, out_shape=jax.ShapeDtypeStruct(cpl.shape, BF16), i...]
where the time goes in v4:
time: 63.3 us; the launch traced here: 62.7 us
  Pallas kernels  60.8 us (96%)
  local copies, waits for them, and re-layouts  1.89 us (3%)
    pallas_call x1, Pallas kernels, on_device(): pl.pallas_call(kernel, out_shape=jax.ShapeDtypeStruct(cpl.shape, BF16), i...  60.8 us
    unnamed x1, local copies, waits for them, and re-layouts  1.89 us

profile of v4, /device:TPU:1, one launch (start us, length us, event | category | flops | bytes accessed | tf_op | source)
XLA Modules:
  0.0 62.7 jit_solution(4965049875870899106)
XLA Ops:
  0.0 60.8 %shard_map.91 = bf16[16,128,128]{2,1,0:T(8,128)(2,1)} custom-call(bf16[8,128,256]{2,1,0:T(8,128)(2,1)} %x_hbm.1, bf16[16,128,128]{2,1,0:T(8,128)(2,1)} %cpl_hbm.1, f32[1,256]{1,0:T(1,128)} %bitcast.6, bf16[32,256]{1,0:T(8,128)(2,1)} %bitcast.4, bf16[32,256]{1,0:T(8,128)(2,1)} %bitcast.5, bf16[1024,128]{1,0:T(8,128)(2,1)} %w3_hbm.1, f32[1,128]{1,0:T(1,128)} %bitcast.7, ...), custom_call_target="tpu_custom_call" | custom-call | tf_op jit(solution)/shard_map/pallas_call | solution.py:584
  60.8 1.9 %copy.11 = bf16[16,128,128]{2,1,0:T(8,128)(2,1)} copy(bf16[16,128,128]{2,1,0:T(8,128)(2,1)} %shard_map.91) | data formatting | bytes 1048576

commit v5 on v4

--- a/solution.py
+++ b/solution.py
@@ -174,8 +174,8 @@
             device_id_type=MESH,
         )
 
+    swap(1).start()
     swap(0).start()
-    swap(1).start()
     xr_ref[core] = rx_ref[pl.ds(pl.multiple_of(core * 128, 128), 128), :]
     xl_ref[core] = lx_ref[core]
 
@@ -269,151 +269,6 @@
     def sent(copy):
         copy.wait_send()
 
-    mine = zh * 16 + x * 4 + y
-    swap_in(0).wait_recv()
-    for q in range(16):
-        rb_ref[core, mine, :, q * 128 : (q + 1) * 128] = jnp.concatenate(
-            [xr_ref[0, q * 8 : (q + 1) * 8, :], xr_ref[1, q * 8 : (q + 1) * 8, :]], axis=0
-        ).astype(BF16)
-
-    def at(da, db):
-        px = (x + da * (1 - core) + db * core + 4) % 4
-        py = (y + da * core + db * (1 - core) + 4) % 4
-        return px, py
-
-    def slot_of(da, db, hh):
-        px, py = at(da, db)
-        return hh * 16 + px * 4 + py
-
-    def dev_of(da, db):
-        px, py = at(da, db)
-        return (rows_of(px, py, zh, core), zl)
-
-    def rblocks(count, sem):
-        return pltpu.make_async_remote_copy(
-            src_ref=rb_ref.at[core, pl.ds(0, count)],
-            dst_ref=rb_ref.at[core, pl.ds(0, count)],
-            send_sem=rsend.at[0],
-            recv_sem=rrecv.at[sem],
-            device_id=sib,
-            device_id_type=MESH,
-        )
-
-    def rfull(slot, dev, sem):
-        return pltpu.make_async_remote_copy(
-            src_ref=rb_ref.at[core, slot],
-            dst_ref=rb_ref.at[core, slot],
-            send_sem=rsend.at[0],
-            recv_sem=rrecv.at[sem],
-            device_id=dev,
-            device_id_type=MESH,
-        )
-
-    def rhalf(slot, part, dev, sem):
-        piece = rb_ref.at[core, slot, :, pl.ds(part * 1024, 1024)]
-        return pltpu.make_async_remote_copy(
-            src_ref=piece,
-            dst_ref=piece,
-            send_sem=rsend.at[0],
-            recv_sem=rrecv.at[sem],
-            device_id=dev,
-            device_id_type=MESH,
-        )
-
-    def scopy(slot):
-        return pltpu.make_async_remote_copy(
-            src_ref=rb_ref.at[core, slot],
-            dst_ref=rb_ref.at[core, slot],
-            send_sem=sibsend.at[0],
-            recv_sem=sibrecv.at[0],
-            device_id=sib,
-            device_id_type=MESH,
-        )
-
-    steps = (0, -1, 1, 2)
-
-    def begin(hh):
-        slot = slot_of(0, 0, hh)
-        for da, db, sem in ((1, 0, 0), (-1, 0, 1), (0, 1, 3), (0, -1, 4)):
-            rfull(slot, dev_of(da, db), sem).start()
-        scopy(slot).start()
-
-    def to_b(slot, n):
-        rfull(slot, dev_of(0, 1), 3 + 2 * n).start()
-        rfull(slot, dev_of(0, -1), 4 + 2 * n).start()
-        scopy(slot).start()
-
-    def ring_a(hh):
-        for part in range(2):
-            step = 1 - 2 * part
-            slot = slot_of(-step, 0, hh)
-            rblocks(1, part).wait_recv()
-            rhalf(slot, part, dev_of(step, 0), 2).start()
-            to_b(slot, 1 + part)
-
-    def ring_a_far(hh):
-        rblocks(1, 2).wait_recv()
-        to_b(slot_of(2, 0, hh), 3)
-
-    def ring_b(hh, n):
-        for part in range(2):
-            step = 1 - 2 * part
-            slot = slot_of(steps[n], -step, hh)
-            rblocks(1, 3 + 2 * n + part).wait_recv()
-            rhalf(slot, part, dev_of(0, step), 11).start()
-            scopy(slot).start()
-
-    def ring_b_far(hh):
-        rblocks(4, 11).wait_recv()
-        for n in range(4):
-            scopy(slot_of(steps[n], 2, hh)).start()
-
-    def begin_straight(hh):
-        slot = slot_of(0, 0, hh)
-        for step, sem in ((1, 13), (-1, 14), (2, 15)):
-            rfull(slot, dev_of(step, 0), sem).start()
-        for step in (1, -1, 2):
-            rfull(slot, dev_of(0, step), 16).start()
-        scopy(slot).start()
-
-    def ring_a_straight(hh):
-        for n in range(1, 4):
-            slot = slot_of(steps[n], 0, hh)
-            rblocks(1, 12 + n).wait_recv()
-            for step in (1, -1, 2):
-                rfull(slot, dev_of(0, step), 16 + n).start()
-            scopy(slot).start()
-
-    def ring_b_straight(hh, n):
-        rblocks(3, 16 + n).wait_recv()
-        for db in (-1, 1, 2):
-            scopy(slot_of(steps[n], db, hh)).start()
-
-
-    def rout(part):
-        return pltpu.make_async_remote_copy(
-            src_ref=rb_ref.at[core, mine, :, pl.ds(part * 1024, 1024)],
-            dst_ref=ry_ref.at[part],
-            send_sem=rysend.at[part],
-            recv_sem=ryrecv.at[part],
-            device_id=zdev(4 - 8 * part),
-            device_id_type=MESH,
-        )
-
-    def ron(part):
-        slot = half_of(z - 4 + 8 * part) * 16 + x * 4 + y
-        return pltpu.make_async_remote_copy(
-            src_ref=ry_ref.at[part],
-            dst_ref=rb_ref.at[core, slot, :, pl.ds(part * 1024, 1024)],
-            send_sem=rysend.at[2 + part],
-            recv_sem=rrecv.at[12],
-            device_id=zdev(4 - 8 * part),
-            device_id_type=MESH,
-        )
-
-    rout(0).start()
-    rout(1).start()
-    begin(zh)
     swap_in(1).wait_recv()
     for hy in range(4):
         for g in range(4):
@@ -423,6 +278,152 @@
             ).astype(BF16)
     for way in range(2):
         zput(way, 1, start)
+
+    mine = zh * 16 + x * 4 + y
+    swap_in(0).wait_recv()
+    for q in range(16):
+        rb_ref[core, mine, :, q * 128 : (q + 1) * 128] = jnp.concatenate(
+            [xr_ref[0, q * 8 : (q + 1) * 8, :], xr_ref[1, q * 8 : (q + 1) * 8, :]], axis=0
+        ).astype(BF16)
+
+    def at(da, db):
+        px = (x + da * (1 - core) + db * core + 4) % 4
+        py = (y + da * core + db * (1 - core) + 4) % 4
+        return px, py
+
+    def slot_of(da, db, hh):
+        px, py = at(da, db)
+        return hh * 16 + px * 4 + py
+
+    def dev_of(da, db):
+        px, py = at(da, db)
+        return (rows_of(px, py, zh, core), zl)
+
+    def rblocks(count, sem):
+        return pltpu.make_async_remote_copy(
+            src_ref=rb_ref.at[core, pl.ds(0, count)],
+            dst_ref=rb_ref.at[core, pl.ds(0, count)],
+            send_sem=rsend.at[0],
+            recv_sem=rrecv.at[sem],
+            device_id=sib,
+            device_id_type=MESH,
+        )
+
+    def rfull(slot, dev, sem):
+        return pltpu.make_async_remote_copy(
+            src_ref=rb_ref.at[core, slot],
+            dst_ref=rb_ref.at[core, slot],
+            send_sem=rsend.at[0],
+            recv_sem=rrecv.at[sem],
+            device_id=dev,
+            device_id_type=MESH,
+        )
+
+    def rhalf(slot, part, dev, sem):
+        piece = rb_ref.at[core, slot, :, pl.ds(part * 1024, 1024)]
+        return pltpu.make_async_remote_copy(
+            src_ref=piece,
+            dst_ref=piece,
+            send_sem=rsend.at[0],
+            recv_sem=rrecv.at[sem],
+            device_id=dev,
+            device_id_type=MESH,
+        )
+
+    def scopy(slot):
+        return pltpu.make_async_remote_copy(
+            src_ref=rb_ref.at[core, slot],
+            dst_ref=rb_ref.at[core, slot],
+            send_sem=sibsend.at[0],
+            recv_sem=sibrecv.at[0],
+            device_id=sib,
+            device_id_type=MESH,
+        )
+
+    steps = (0, -1, 1, 2)
+
+    def begin(hh):
+        slot = slot_of(0, 0, hh)
+        for da, db, sem in ((1, 0, 0), (-1, 0, 1), (0, 1, 3), (0, -1, 4)):
+            rfull(slot, dev_of(da, db), sem).start()
+        scopy(slot).start()
+
+    def to_b(slot, n):
+        rfull(slot, dev_of(0, 1), 3 + 2 * n).start()
+        rfull(slot, dev_of(0, -1), 4 + 2 * n).start()
+        scopy(slot).start()
+
+    def ring_a(hh):
+        for part in range(2):
+            step = 1 - 2 * part
+            slot = slot_of(-step, 0, hh)
+            rblocks(1, part).wait_recv()
+            rhalf(slot, part, dev_of(step, 0), 2).start()
+            to_b(slot, 1 + part)
+
+    def ring_a_far(hh):
+        rblocks(1, 2).wait_recv()
+        to_b(slot_of(2, 0, hh), 3)
+
+    def ring_b(hh, n):
+        for part in range(2):
+            step = 1 - 2 * part
+            slot = slot_of(steps[n], -step, hh)
+            rblocks(1, 3 + 2 * n + part).wait_recv()
+            rhalf(slot, part, dev_of(0, step), 11).start()
+            scopy(slot).start()
+
+    def ring_b_far(hh):
+        rblocks(4, 11).wait_recv()
+        for n in range(4):
+            scopy(slot_of(steps[n], 2, hh)).start()
+
+    def begin_straight(hh):
+        slot = slot_of(0, 0, hh)
+        for step, sem in ((1, 13), (-1, 14), (2, 15)):
+            rfull(slot, dev_of(step, 0), sem).start()
+        for step in (1, -1, 2):
+            rfull(slot, dev_of(0, step), 16).start()
+        scopy(slot).start()
+
+    def ring_a_straight(hh):
+        for n in range(1, 4):
+            slot = slot_of(steps[n], 0, hh)
+            rblocks(1, 12 + n).wait_recv()
+            for step in (1, -1, 2):
+                rfull(slot, dev_of(0, step), 16 + n).start()
+            scopy(slot).start()
+
+    def ring_b_straight(hh, n):
+        rblocks(3, 16 + n).wait_recv()
+        for db in (-1, 1, 2):
+            scopy(slot_of(steps[n], db, hh)).start()
+
+
+    def rout(part):
+        return pltpu.make_async_remote_copy(
+            src_ref=rb_ref.at[core, mine, :, pl.ds(part * 1024, 1024)],
+            dst_ref=ry_ref.at[part],
+            send_sem=rysend.at[part],
+            recv_sem=ryrecv.at[part],
+            device_id=zdev(4 - 8 * part),
+            device_id_type=MESH,
+        )
+
+    def ron(part):
+        slot = half_of(z - 4 + 8 * part) * 16 + x * 4 + y
+        return pltpu.make_async_remote_copy(
+            src_ref=ry_ref.at[part],
+            dst_ref=rb_ref.at[core, slot, :, pl.ds(part * 1024, 1024)],
+            send_sem=rysend.at[2 + part],
+            recv_sem=rrecv.at[12],
+            device_id=zdev(4 - 8 * part),
+            device_id_type=MESH,
+        )
+
+    rout(0).start()
+    rout(1).start()
+    begin(zh)
     spread(z)
 
     loads[4].wait()
@@ -444,11 +445,11 @@
 
     other = 1 - zh
     ring_a(zh)
+    zstep(1)
     ring_b(zh, 0)
     for part in range(2):
         rout(part).wait_recv()
         ron(part).start()
-    zstep(1)
     ring_a_far(zh)
     zstep(2)
     ring_b(zh, 1)
@@ -458,8 +459,8 @@
     begin_straight(other)
     ring_b(zh, 3)
     zstep(4)
+    zstep(5)
     ring_a_straight(other)
-    zstep(5)
     ring_b_far(zh)
     zstep(6)
     ring_b_straight(other, 0)

time: 63.3 us -> 61.7 us (0.975)
  Pallas kernels: 60.8 us -> 58.9 us
    pallas_call x1, Pallas kernels: 60.8 us -> 58.9 us  [on_device(): pl.pallas_call(kernel, out_shape=jax.ShapeDtypeStruct(cpl.shape, BF16), i...]
where the time goes in v5:
time: 61.7 us; the launch traced here: 60.8 us
  Pallas kernels  58.9 us (95%)
  local copies, waits for them, and re-layouts  1.89 us (3%)
    pallas_call x1, Pallas kernels, on_device(): pl.pallas_call(kernel, out_shape=jax.ShapeDtypeStruct(cpl.shape, BF16), i...  58.9 us
    unnamed x1, local copies, waits for them, and re-layouts  1.89 us

profile of v5, /device:TPU:1, one launch (start us, length us, event | category | flops | bytes accessed | tf_op | source)
XLA Modules:
  0.0 60.8 jit_solution(65634383490024394)
XLA Ops:
  0.0 58.9 %shard_map.91 = bf16[16,128,128]{2,1,0:T(8,128)(2,1)} custom-call(bf16[8,128,256]{2,1,0:T(8,128)(2,1)} %x_hbm.1, bf16[16,128,128]{2,1,0:T(8,128)(2,1)} %cpl_hbm.1, f32[1,256]{1,0:T(1,128)} %bitcast.6, bf16[32,256]{1,0:T(8,128)(2,1)} %bitcast.4, bf16[32,256]{1,0:T(8,128)(2,1)} %bitcast.5, bf16[1024,128]{1,0:T(8,128)(2,1)} %w3_hbm.1, f32[1,128]{1,0:T(1,128)} %bitcast.7, ...), custom_call_target="tpu_custom_call" | custom-call | tf_op jit(solution)/shard_map/pallas_call | solution.py:585
  58.9 1.9 %copy.11 = bf16[16,128,128]{2,1,0:T(8,128)(2,1)} copy(bf16[16,128,128]{2,1,0:T(8,128)(2,1)} %shard_map.91) | data formatting | bytes 1048576
